TPU v7x, 32 devices: a whole 2x2x4 slice. The times are simulated.
32 devices in a mesh: corpus: 16 (over z, y, x), batch: 2 (over core).
Axes of the slice: x: 2, y: 2, z: 4, core: 2. Of those that a mesh axis runs over, the one named last changes fastest.
Arguments:
- queries: float32 [128, 1024], P(('corpus', 'batch')), may hold values from -6.25 to 6.25, as said below
- codes: int32 [98304, 32], P('corpus'), may hold values from -2147483648 to 2147483647
- quant_rows: bfloat16 [98304, 1024], P('corpus'), may hold values from -127 to 127, as said below
- row_scale: float32 [98304], P('corpus'), may hold values from 0.0005 to 0.002
- candidates: int32 [128, 40], P(('corpus', 'batch')), may hold values from 0 to 98303
- shortlist: int32 [128], P(('corpus', 'batch')), may hold values from 1 to 40
- edges: int32 [17], replicated, may hold values from 464 to 563, as said below
Outputs:
- hist: float32 [128, 16], P(('corpus', 'batch'))
- scores: float32 [128, 40], P(('corpus', 'batch'))
Inputs may be any that keep to these rules, and one draw needn't show every extreme that they name: `queries`: no entry lies within 0.25 of zero. `quant_rows`: whole numbers. `edges`: strictly increasing.
All inputs are finite; a program needn't handle non-finite values.
Results may differ from a plain program's by a relative error of at most 0.0003.
Values sent between devices are 32-bit elements; how exact they have to be, the bound alone decides.
No kernel may reach another device: no remote copies, remote signals or barrier semaphores. Data moves between devices by JAX's collectives and lax.ppermute only.
A program may use at most 64 MiB of HBM per device.

v0:
```python
import math

import jax
import jax.numpy as jnp
from jax import lax
from jax.sharding import PartitionSpec as P


def unpack(words):
    bits = jnp.right_shift(words[..., None], jnp.arange(32, dtype=jnp.int32)) & 1
    signed = (2 * bits - 1).reshape(words.shape[:-1] + (words.shape[-1] * 32,))
    return signed.astype(jnp.bfloat16)


def histogram(queries, codes, edges, width):
    count_q = queries.shape[0]
    count_rows = codes.shape[0]
    signs = jnp.where(queries >= 0, 1.0, -1.0).astype(jnp.bfloat16)
    limits = edges.astype(jnp.float32)
    block = math.gcd(count_rows, 1024)

    def step(total, number):
        words = lax.dynamic_slice_in_dim(codes, number * block, block, 0)
        plus = unpack(words)
        inner = jnp.dot(signs, plus.T, preferred_element_type=jnp.float32)
        ham = (width - inner) * 0.5
        above = jnp.stack(
            [
                jnp.sum((ham >= limits[k]).astype(jnp.float32), axis=1)
                for k in range(limits.shape[0])
            ],
            axis=1,
        )
        return (total + above, None)

    start_total = jnp.zeros((count_q, limits.shape[0]), jnp.float32)
    above, _ = lax.scan(step, start_total, jnp.arange(count_rows // block, dtype=jnp.int32))
    return above[:, :-1] - above[:, 1:]


def rescore(queries, quant_rows, row_scale, lists, lengths, base, first, span):
    count_rows = quant_rows.shape[0]
    count_q, cand = lists.shape
    total_slots = count_q * cand
    group = 512
    local = lists - base
    slot_ids = jnp.arange(cand, dtype=jnp.int32)
    live = (local >= first) & (local < first + span) & (slot_ids[None, :] < lengths[:, None])
    flat_live = live.reshape(-1)
    flat_target = jnp.clip(local, 0, count_rows - 1).reshape(-1)
    rank = jnp.cumsum(flat_live.astype(jnp.int32)) - 1
    place = jnp.where(flat_live, rank, total_slots + group)
    order = (
        jnp.zeros((total_slots + group,), jnp.int32)
        .at[place]
        .set(jnp.arange(total_slots, dtype=jnp.int32), mode="drop")
    )
    found = jnp.sum(flat_live.astype(jnp.int32))
    trips = (found + group - 1) // group
    lanes = jnp.arange(group, dtype=jnp.int32)

    def visit(number, flat_scores):
        picked = lax.dynamic_slice_in_dim(order, number * group, group, 0)
        valid = number * group + lanes < found
        owner = picked // cand
        target = flat_target[picked]
        values = (
            jnp.sum(queries[owner] * quant_rows[target].astype(jnp.float32), axis=1)
            * row_scale[target]
        )
        spot = jnp.where(valid, picked, total_slots)
        return flat_scores.at[spot].set(values, mode="drop")

    flat = lax.fori_loop(0, trips, visit, jnp.zeros((total_slots,), jnp.float32))
    return flat.reshape(count_q, cand)


def shards(queries, codes, quant_rows, row_scale, candidates, shortlist, edges):
    count_rows = codes.shape[0]
    width = quant_rows.shape[1]
    total = count_rows * lax.axis_size("corpus")
    base = lax.axis_index("corpus") * count_rows
    every = lax.all_gather(queries, ("corpus", "batch"), axis=0, tiled=True)
    lists, lengths = (
        lax.all_gather(candidates, ("corpus", "batch"), axis=0, tiled=True),
        lax.all_gather(shortlist, ("corpus", "batch"), axis=0, tiled=True),
    )
    span = count_rows // lax.axis_size("batch")
    first = lax.axis_index("batch") * span
    own_codes = lax.dynamic_slice_in_dim(codes, first, span, 0)
    counts = histogram(every, own_codes, edges, width)
    scores = rescore(every, quant_rows, row_scale, lists, lengths, base, first, span)
    counts, scores = (
        lax.psum_scatter(counts, ("corpus", "batch"), scatter_dimension=0, tiled=True),
        lax.psum_scatter(scores, ("corpus", "batch"), scatter_dimension=0, tiled=True),
    )
    nbins = edges.shape[0] - 1
    hist = counts * (nbins / total)
    return (hist, scores)


def solution(mesh):
    return jax.shard_map(
        shards,
        mesh=mesh,
        in_specs=(
            P(("corpus", "batch"), None),
            P("corpus", None),
            P("corpus", None),
            P("corpus"),
            P(("corpus", "batch"), None),
            P(("corpus", "batch")),
            P(),
        ),
        out_specs=(P(("corpus", "batch"), None), P(("corpus", "batch"), None)),
        check_vma=False,
    )
```

profile of v0, /device:TPU:0, one launch (start us, length us, event | category | flops | bytes accessed | tf_op | source)
XLA Modules:
  0.0 254.0 jit_solution(11925215523051765266)
XLA Ops:
  0.6 0.0 copy-start
  0.6 0.0 copy-start.1
  0.7 43.8 %all-gather.1 = s32[32,4,40]{2,1,0:T(4,128)S(1)} all-gather(s32[1,4,40]{2,1,0:T(4,128)} %bitcast.157), channel_id=1, replica_groups=mesh['corpus'=16,'batch'=2] {'corpus','batch'}, dimensions={0}, use_global_device_ids=true | all-gather | bytes 21120 | tf_op jit(solution)/shard_map/all_gather | solution.py:85
  44.5 0.9 dynamic-update-slice
  45.4 36.8 %all-reduce = s32[128]{0:T(128)S(1)} all-reduce(s32[128]{0:T(128)S(1)} %dynamic-update-slice), channel_id=1, replica_groups=mesh['corpus'=16,'batch'=2] {'corpus','batch'}, use_global_device_ids=true, to_apply=%add | all-reduce | flops 128 | bytes 1024
  82.2 0.1 fusion.12
  82.3 0.6 convert_reduce_fusion.17
  83.6 0.1 reshape.102
  83.7 0.3 reduce-window.9
  84.0 0.1 slice.144
  84.1 0.1 reduce-window.12
  84.1 0.1 slice_reduce_fusion
  84.3 0.1 add_add_fusion
  84.3 0.1 reshape.98
  84.5 19.3 %scatter_custom_fusion.1 = s32[5632]{0:T(1024)S(1)} fusion(s32[5120]{0:T(1024)S(1)} %bitcast.138, s32[5120]{0:T(1024)S(1)} %iota.22, s32[]{:T(128)} %constant.146.clone.1), kind=kCustom, calls=%fused_computation.56 | custom fusion | bytes 22532 | tf_op jit(solution)/shard_map/scatter | solution.py:56
  103.8 0.1 reshape.100
  104.0 41.8 %all-gather = f32[32,4,1024]{2,1,0:T(4,128)S(1)} all-gather(f32[1,4,1024]{2,1,0:T(4,128)} %bitcast.139), channel_id=1, replica_groups=mesh['corpus'=16,'batch'=2] {'corpus','batch'}, dimensions={0}, use_global_device_ids=true | all-gather | bytes 540672 | tf_op jit(solution)/shard_map/all_gather | solution.py:83
  145.8 0.2 reshape.157
  146.0 0.0 copy-done.1
  146.0 0.0 copy-start.2
  146.0 22.9 %while.26 = (s32[]{:T(128)}, f32[5120]{0:T(1024)S(1)}, s32[]{:T(128)}, s32[]{:T(128)}, s32[5632]{0:T(1024)S(1)}, /*index=5*/f32[128,1024]{1,0:T(8,128)S(1)}, s32...) while((s32[]{:T(128)}, f32[5120]{0:T(1024)S(1)}, ...), condition=%wide.region_27.28_spmd.clone, body=%wide.region_24.27_spmd.clone.sunk | while | flops 1587718 | bytes 9500855 | solution.py:74
  146.1 0.7 compare_select_fusion.7
  146.8 3.1 %gather_fusion.1 = s32[512]{0:T(512)S(1)} fusion(s32[5120]{0:T(1024)S(1)} %get-tuple-element.558, s32[1024]{0:T(1024)S(1)} %get-tuple-element.455), kind=kCustom, calls=%fused_computation.1.clone.clone.1 | custom fusion | bytes 6144 | tf_op jit(solution)/shard_map/while/body/gather | solution.py:66
  150.0 9.7 %gather_fusion.2 = bf16[512,1024]{1,0:T(8,128)(2,1)} fusion(bf16[6144,1024]{1,0:T(8,128)(2,1)} %get-tuple-element.559, s32[1024]{0:T(1024)S(1)} %pad_clamp_fusion.6), kind=kCustom, calls=%fused_computation.2.clone.clone.1 | custom fusion | bytes 2099200 | tf_op jit(solution)/shard_map/while/body/gather | solution.py:68
  159.7 1.9 gather_fusion
  161.6 1.5 multiply_reduce_fusion.2
  163.1 3.1 %gather_fusion.3 = f32[512]{0:T(512)S(1)} fusion(f32[6144]{0:T(1024)S(1)} %get-tuple-element.560, s32[1024]{0:T(1024)S(1)} %pad_clamp_fusion.6), kind=kCustom, calls=%fused_computation.3.clone.clone.1 | custom fusion | bytes 6144 | tf_op jit(solution)/shard_map/while/body/gather | solution.py:69
  166.2 2.5 scatter_fusion
  168.9 0.1 reshape.101
  169.0 0.0 copy-done
  169.1 0.0 copy-done.2
  169.2 45.6 %while.27 = (s32[]{:T(128)}, f32[128,17]{0,1:T(8,128)S(1)}, s32[3]{0:T(128)S(1)}, s32[3072,32]{0,1:T(8,128)S(1)}, bf16[128,1024]{1,0:T(8,128)(2,1)S(1)}, /*index...) while((s32[]{:T(128)}, f32[128,17]{0,1:T(8,128)S(1)}, s32[3]{0:T(128)S(1)}, ...), condition=%wide.region_18.19_spmd.clone, body=%wide.region_0.18_spmd.clone.sunk | while | flops 280627328 | bytes 4918649 | solution.py:37
  169.2 0.6 dynamic_slice.36
  170.5 0.1 shift_right_arithmetic.49
  170.5 0.8 fusion.24
  171.4 0.7 fusion.23
  172.1 12.2 %convert_reduce_fusion.19 = (f32[128]{0:T(128)S(1)}, f32[128]{0:T(128)S(1)}, f32[128]{0:T(128)S(1)}, f32[128]{0:T(128)S(1)}, f32[128]{0:T(128)S(1)}, /*index=5*/...) fusion(f32[]{:T(128)} %bitcast.99, ...), kind=kOutput, calls=%fused_computation.28.clone.1 | convolution fusion | flops 275380096 | bytes 2368068 | tf_op jit(solution)/shard_map/while/body/eval_jaxpr/dot_general | solution.py:25
  184.3 0.1 stack.127
  184.4 0.6 dynamic_slice.36
  185.7 0.1 shift_right_arithmetic.49
  185.7 0.8 fusion.24
  186.6 0.7 fusion.23
  187.3 12.2 %convert_reduce_fusion.19 = (f32[128]{0:T(128)S(1)}, f32[128]{0:T(128)S(1)}, f32[128]{0:T(128)S(1)}, f32[128]{0:T(128)S(1)}, f32[128]{0:T(128)S(1)}, /*index=5*/...) fusion(f32[]{:T(128)} %bitcast.99, ...), kind=kOutput, calls=%fused_computation.28.clone.1 | convolution fusion | flops 275380096 | bytes 2368068 | tf_op jit(solution)/shard_map/while/body/eval_jaxpr/dot_general | solution.py:25
  199.5 0.1 stack.127
  199.6 0.6 dynamic_slice.36
  200.9 0.1 shift_right_arithmetic.49
  200.9 0.8 fusion.24
  201.8 0.7 fusion.23
  202.5 12.2 %convert_reduce_fusion.19 = (f32[128]{0:T(128)S(1)}, f32[128]{0:T(128)S(1)}, f32[128]{0:T(128)S(1)}, f32[128]{0:T(128)S(1)}, f32[128]{0:T(128)S(1)}, /*index=5*/...) fusion(f32[]{:T(128)} %bitcast.99, ...), kind=kOutput, calls=%fused_computation.28.clone.1 | convolution fusion | flops 275380096 | bytes 2368068 | tf_op jit(solution)/shard_map/while/body/eval_jaxpr/dot_general | solution.py:25
  214.7 0.1 stack.127
  214.8 0.1 copy.16
  214.9 37.9 %all-reduce.3 = (f32[128,16]{1,0:T(8,128)S(1)}, f32[128,40]{1,0:T(8,128)S(1)}) all-reduce(f32[128,16]{1,0:T(8,128)S(1)} %copy.16, f32[128,40]{1,0:T(8,128)S(1)} %reshape.101), channel_id=2, replica_groups=mesh['corpus'=16,'batch'=2] {'corpus','batch'}, use_global_device_ids=true, to_apply=%region_19.20.clone | all-reduce | flops 7168 | bytes 57344
  252.8 0.6 constant_dynamic-slice_fusion.1
  253.4 0.6 dynamic-slice_multiply_fusion
  (25 shorter events, 0.3 us)
Async XLA Ops:
  0.6 168.4 %copy-start = (s32[6144,32]{0,1:T(8,128)S(1)}, s32[6144,32]{0,1:T(8,128)}, u32[]{:S(2)}) copy-start(s32[6144,32]{0,1:T(8,128)} %param.12) | copy-start | bytes 2359300
  0.6 145.4 %copy-start.1 = (f32[6144]{0:T(1024)S(1)}, f32[6144]{0:T(1024)}, u32[]{:S(2)}) copy-start(f32[6144]{0:T(1024)} %param.14) | copy-start | bytes 73732
  146.0 23.1 %copy-start.2 = (s32[17]{0:T(128)S(1)}, s32[17]{0:T(128)}, u32[]{:S(2)}) copy-start(s32[17]{0:T(128)} %param.17) | copy-start | bytes 208
where the time goes:
time: 256 us; the launch traced here: 254 us
  blocking collectives  160 us (62%)
  local copies, waits for them, and re-layouts  46.4 us (18%)
  matrix products  36.6 us (14%)
  other arithmetic  6.64 us (3%)
    unnamed x2, blocking collectives  74.7 us
    all_gather x1, blocking collectives, shards(): lax.all_gather(candidates, ('corpus', 'batch'), axis=0, tiled=True)  43.8 us
    all_gather x1, blocking collectives, shards(): every = lax.all_gather(queries, ('corpus', 'batch'), axis=0, tiled=True)  41.8 us
    dot_general x3, matrix products, step(): inner = jnp.dot(signs, plus.T, preferred_element_type=jnp.float32)  36.6 us
    scatter x1, local copies, waits for them, and re-layouts, rescore(): order = jnp.zeros((total_slots + group,), jnp.int32).at[place].set(jnp.ar...  19.3 us
    gather x1, local copies, waits for them, and re-layouts, visit(): quant_rows[target].astype(jnp.float32)  9.68 us

commit v1 on v0

v1 whole, which is shorter than its diff:
```python
import functools

import jax
import jax.numpy as jnp
from jax import lax
from jax.experimental import pallas as pl
from jax.experimental.pallas import tpu as pltpu
from jax.sharding import PartitionSpec as P

LANES = 128
F32, BF16, I32, I16 = jnp.float32, jnp.bfloat16, jnp.int32, jnp.int16


def pack_kernel(peers, q_ref, cand_ref, len_ref, out_ref):
    own, width = q_ref.shape
    slots = cand_ref.shape[1]
    vregs = width // LANES
    rows = out_ref.shape[0] // peers
    lens = len_ref[...]
    cand = cand_ref[...]
    slot = lax.broadcasted_iota(I32, cand.shape, 1)
    wide = jnp.where(slot < lens, cand, -1).astype(F32)
    wide = jnp.concatenate([wide, jnp.full((own, LANES - slots), -1.0, F32)], axis=1)
    parts = [q_ref[i : i + 1, v * LANES : (v + 1) * LANES] for i in range(own) for v in range(vregs)]
    parts.append(wide)
    fill = rows - own * vregs - own
    parts.append(jnp.zeros((fill, LANES), F32))
    block = jnp.concatenate(parts, axis=0)
    for p in range(peers):
        out_ref[p * rows : (p + 1) * rows, :] = block


def main_kernel(peers, own, width, slots, nedges, base_ref, edges_ref, x_ref, codes_ref, quant_ref, scale_ref, out_ref, signs_s, qhl_s, bits_s, idx_s, cnt_s, sc_s, inner_s):
    step = pl.program_id(0)
    steps = pl.num_programs(0)
    nq = peers * own
    vregs = width // LANES
    rows = x_ref.shape[0] // peers
    chunk = quant_ref.shape[0]
    words = codes_ref.shape[1]
    reps = LANES // words

    @pl.when(step == 0)
    def _():
        d = lax.broadcasted_iota(I32, (width, 1), 0)
        w, k = d // 32, d % 32
        h, t, c = k // 16, (k % 16) // reps, k % reps
        dest = h * (width // 2) + t * LANES + c * words + w
        plain = []
        for ql in range(own):
            row = jnp.concatenate(
                [x_ref[pl.ds(ql * vregs + v, peers, stride=rows), :] for v in range(vregs)], axis=1
            )
            plain.append(row)
            hi = row.astype(BF16)
            lo = (row - hi.astype(F32)).astype(BF16)
            qhl_s[ql * peers : (ql + 1) * peers, :] = hi
            qhl_s[nq + ql * peers : nq + (ql + 1) * peers, :] = lo
            idx = x_ref[pl.ds(own * vregs + ql, peers, stride=rows), :].astype(I32)
            idx_s[ql * peers : (ql + 1) * peers, :] = jnp.where(idx < 0, -1, idx - base_ref[0])
        full = jnp.concatenate(plain, axis=0)
        signs = jnp.where(full >= 0, 1.0, -1.0).astype(BF16)
        for j in range(width // LANES):
            lane = lax.broadcasted_iota(I32, (1, LANES), 1) + j * LANES
            perm = jnp.where(dest == lane, 1.0, 0.0).astype(BF16)
            signs_s[:, j * LANES : (j + 1) * LANES] = jnp.dot(
                signs, perm, preferred_element_type=F32
            ).astype(BF16)
        cnt_s[...] = jnp.zeros(cnt_s.shape, I16)
        sc_s[...] = jnp.zeros(sc_s.shape, F32)

    lane = lax.broadcasted_iota(I32, (1, LANES), 1)
    sub = lane // words
    word = codes_ref[...]
    tiled = jnp.concatenate([word] * reps, axis=1)
    halves = (tiled.astype(I16), lax.shift_right_logical(tiled, 16).astype(I16))
    for h in range(2):
        for t in range(16 // reps):
            bit = jnp.left_shift(1, t * reps + sub)
            mask = jnp.broadcast_to(bit, (16, LANES)).astype(I16)
            mask = jnp.concatenate([mask] * (chunk // 16), axis=0)
            on = (halves[h] & mask) != 0
            col = h * (width // 2) + t * LANES
            bits_s[:, col : col + LANES] = jnp.where(on, BF16(1), BF16(-1))
    inner = lax.dot_general(
        signs_s[...], bits_s[...], (((1,), (1,)), ((), ())), preferred_element_type=F32
    )
    inner_s[...] = inner.astype(I32).astype(I16)
    for g in range(nq // 16):
        cols = [inner_s[g * 16 : (g + 1) * 16, j * LANES : (j + 1) * LANES] for j in range(chunk // LANES)]
        for k in range(nedges):
            thr = jnp.full((16, LANES), width - 2 * edges_ref[k], I32).astype(I16)
            tot = None
            for x in cols:
                one = jnp.where(x <= thr, I16(1), I16(0))
                tot = one if tot is None else tot + one
            cnt_s[k, g * 16 : (g + 1) * 16, :] += tot
    prod = lax.dot_general(
        qhl_s[...], quant_ref[...], (((1,), (1,)), ((), ())), preferred_element_type=F32
    )
    idx = idx_s[...]
    low = idx & (LANES - 1)
    high = idx >> 7
    acc = sc_s[...]
    for j in range(chunk // LANES):
        s = (prod[:nq, j * LANES : (j + 1) * LANES] + prod[nq:, j * LANES : (j + 1) * LANES]) * scale_ref[:, j * LANES : (j + 1) * LANES]
        got = jnp.take_along_axis(s, low, axis=1, mode="promise_in_bounds")
        acc = jnp.where(high == step * (chunk // LANES) + j, got, acc)
    sc_s[...] = acc

    @pl.when(step == steps - 1)
    def _():
        res = sc_s[...]
        lane = lax.broadcasted_iota(I32, (nq, LANES), 1)
        prev = None
        for k in range(nedges):
            above = jnp.sum(cnt_s[k].astype(I32).astype(F32), axis=1, keepdims=True)
            if k:
                res = jnp.where(lane == LANES // 2 + k - 1, prev - above, res)
            prev = above
        for ql in range(own):
            out_ref[pl.ds(ql, peers, stride=own), :] = res[ql * peers : (ql + 1) * peers, :]


def shards(peers, queries, codes, quant_rows, row_scale, candidates, shortlist, edges):
    own, width = queries.shape
    slots = candidates.shape[1]
    count_rows, words = codes.shape
    nedges = edges.shape[0]
    nbins = nedges - 1
    nq = own * peers
    rows = -(-(own * (width // LANES) + own) // 8) * 8
    chunk = 1024
    payload = pl.pallas_call(
        functools.partial(pack_kernel, peers),
        out_shape=jax.ShapeDtypeStruct((peers * rows, LANES), F32),
        name="pack",
    )(queries, candidates, shortlist.reshape(own, 1))
    got = lax.all_to_all(payload, "corpus", 0, 0, tiled=True)
    base = (lax.axis_index("corpus") * count_rows).astype(I32).reshape(1)
    part = pl.pallas_call(
        functools.partial(main_kernel, peers, own, width, slots, nedges),
        grid=(count_rows // chunk,),
        in_specs=[
            pl.BlockSpec(memory_space=pltpu.SMEM),
            pl.BlockSpec(memory_space=pltpu.SMEM),
            pl.BlockSpec((peers * rows, LANES), lambda i: (0, 0)),
            pl.BlockSpec((chunk, words), lambda i: (i, 0)),
            pl.BlockSpec((chunk, width), lambda i: (i, 0)),
            pl.BlockSpec((1, chunk), lambda i: (0, i)),
        ],
        out_specs=pl.BlockSpec((nq, LANES), lambda i: (0, 0)),
        out_shape=jax.ShapeDtypeStruct((nq, LANES), F32),
        scratch_shapes=[
            pltpu.VMEM((nq, width), BF16),
            pltpu.VMEM((2 * nq, width), BF16),
            pltpu.VMEM((chunk, width), BF16),
            pltpu.VMEM((nq, LANES), I32),
            pltpu.VMEM((nedges, nq, LANES), I16),
            pltpu.VMEM((nq, LANES), F32),
            pltpu.VMEM((nq, chunk), I16),
        ],
        name="main",
    )(base, edges, got, codes, quant_rows, row_scale.reshape(1, count_rows))
    back = lax.all_to_all(part, "corpus", 0, 0, tiled=True)
    total = jnp.sum(back.reshape(peers, own, LANES), axis=0)
    hist = total[:, LANES // 2 : LANES // 2 + nbins] * (nbins / (count_rows * peers))
    return hist, total[:, :slots]


def solution(mesh):
    both = ("corpus", "batch")
    return jax.shard_map(
        functools.partial(shards, mesh.shape["corpus"]),
        mesh=mesh,
        in_specs=(P(both, None), P("corpus", None), P("corpus", None), P("corpus"), P(both, None), P(both), P()),
        out_specs=(P(both, None), P(both, None)),
        check_vma=False,
    )
```

time: 256 us -> 53 us (0.21)
  blocking collectives: 160 us -> 10.9 us
  local copies, waits for them, and re-layouts: 46.4 us -> 5.18 us
  matrix products: 36.6 us -> 0 us
  Pallas kernels: 0 us -> 18.7 us
  starting transfers between devices: 0 us -> 8.34 us
  waiting for transfers between devices: 0 us -> 8.18 us
  other arithmetic: 6.64 us -> 0.68 us
    all_gather x2 -> x0, blocking collectives: 85.7 us -> none  [the longest x1 43.8 us: shards(): lax.all_gather(candidates, ('corpus', 'batch'), axis=0, tiled=True)]
    unnamed x2 -> x0, blocking collectives: 74.7 us -> none
    dot_general x3 -> x0, matrix products: 36.6 us -> none  [step(): inner = jnp.dot(signs, plus.T, preferred_element_type=jnp.float32)]
    scatter x2 -> x0, local copies, waits for them, and re-layouts: 21.8 us -> none  [the longest x1 19.3 us: rescore(): order = jnp.zeros((total_slots + group,), jnp.int32).at[place].set(jnp.ar...]
    pallas_call x0 -> x2, Pallas kernels: none -> 18.7 us  [the longest x1 17.2 us: shards(): pl.pallas_call(functools.partial(main_kernel, peers, own, width, slots, n...]
    gather x4 -> x0, local copies, waits for them, and re-layouts: 17.9 us -> none  [the longest x1 9.68 us: visit(): quant_rows[target].astype(jnp.float32)]
    all_to_all x0 -> x1, blocking collectives: none -> 10.9 us  [shards(): back = lax.all_to_all(part, 'corpus', 0, 0, tiled=True)]
    all_to_all x0 -> x1, starting transfers between devices: none -> 8.34 us  [shards(): got = lax.all_to_all(payload, 'corpus', 0, 0, tiled=True)]
  transfers between devices with their start and end apart: 0 -> 1, of which waited for: 0 -> 1; matrix products, arithmetic and copies ran while one was open for 0% -> 6% of each run, Pallas kernels for 0% -> 0%
where the time goes in v1:
time: 53 us; the launch traced here: 52.6 us
  Pallas kernels  18.7 us (35%)
  blocking collectives  10.9 us (21%)
  starting transfers between devices  8.34 us (16%)
  waiting for transfers between devices  8.18 us (15%)
  local copies, waits for them, and re-layouts  5.18 us (10%)
  other arithmetic  0.68 us (1%)
  between operations  0.65 us (1%)
    pallas_call x1, Pallas kernels, shards(): pl.pallas_call(functools.partial(main_kernel, peers, own, width, slots, n...  17.2 us
    all_to_all x1, blocking collectives, shards(): back = lax.all_to_all(part, 'corpus', 0, 0, tiled=True)  10.9 us
    all_to_all x1, starting transfers between devices, shards(): got = lax.all_to_all(payload, 'corpus', 0, 0, tiled=True)  8.34 us
    all_to_all x1, waiting for transfers between devices, shards(): got = lax.all_to_all(payload, 'corpus', 0, 0, tiled=True)  8.18 us
    unnamed x5, local copies, waits for them, and re-layouts  3.87 us
    pallas_call x1, Pallas kernels, shards(): pl.pallas_call(functools.partial(pack_kernel, peers), out_shape=jax.Shape...  1.54 us
    reshape x1, local copies, waits for them, and re-layouts, shards(): shortlist.reshape(own, 1)  1.31 us
  transfers between devices with their start and end apart: 1, of which 1 were waited for; matrix products, arithmetic and copies ran while one was open for 6% of the time, Pallas kernels for 0%

profile of v1, /device:TPU:0, one launch (start us, length us, event | category | flops | bytes accessed | tf_op | source)
XLA Modules:
  0.0 52.6 jit_solution(8311165935537681294)
XLA Ops:
  0.6 1.3 %copy.9.len_ref = s32[4,1]{1,0:T(4,128)} copy(s32[4,1]{0,1:T(1,128)} %bitcast.12) | data formatting | bytes 32 | tf_op jit(solution)/shard_map/reshape | solution.py:138
  1.9 1.5 %pack.1 = f32[640,128]{1,0:T(8,128)} custom-call(f32[4,1024]{1,0:T(4,128)} %q_ref.1, s32[4,40]{1,0:T(4,128)} %cand_ref.1, s32[4,1]{1,0:T(4,128)} %copy.9.len_ref), custom_call_target="tpu_custom_call" | custom-call | tf_op jit(solution)/shard_map/pack/pallas_call | solution.py:134
  3.5 8.3 %all-to-all-start = ((f32[16,40,128]{2,1,0:T(8,128)}), f32[16,40,128]{2,1,0:T(8,128)S(1)}, u32[]{:S(2)}, u32[]{:S(2)}) async-start(f32[16,40,128]{2,1,0:T(8,128)} %bitcast.7), calls=%async_computation | async-start | bytes 655360 | tf_op jit(solution)/shard_map/all_to_all | solution.py:139
  11.8 3.1 %copy.10.codes_ref = s32[6144,32]{1,0:T(8,128)} copy(s32[6144,32]{0,1:T(8,128)} %param.8) | data formatting | bytes 1572864 | tf_op args[1]
  15.0 8.2 %all-to-all-done = f32[16,40,128]{2,1,0:T(8,128)S(1)} async-done(((f32[16,40,128]{2,1,0:T(8,128)}), f32[16,40,128]{2,1,0:T(8,128)S(1)}, u32[]{:S(2)}, u32[]{:S(2)}) %all-to-all-start) | async-done | bytes 327712 | tf_op jit(solution)/shard_map/all_to_all | solution.py:139
  23.2 0.0 copy-start
  23.2 0.7 %copy-done = f32[16,40,128]{2,1,0:T(8,128)} copy-done((f32[16,40,128]{2,1,0:T(8,128)}, f32[16,40,128]{2,1,0:T(8,128)S(1)}, u32[]{:S(2)}) %copy-start) | copy-done | bytes 327704
  23.9 17.2 %main.1 = f32[64,128]{1,0:T(8,128)} custom-call(s32[1]{0:T(128)} %bitcast.base_ref, s32[17]{0:T(128)} %edges_ref.1, f32[640,128]{1,0:T(8,128)} %bitcast.8, s32[6144,32]{1,0:T(8,128)} %copy.10.codes_ref, bf16[6144,1024]{1,0:T(8,128)(2,1)} %quant_ref.1, f32[1,6144]{1,0:T(1,128)} %bitcast.10), custom_call_target="tpu_custom_call" | custom-call | tf_op jit(solution)/shard_map/main/pallas_call | solution.py:141
  41.1 10.9 %all_to_all.20 = f32[16,4,128]{2,1,0:T(4,128)S(1)} all-to-all(f32[16,4,128]{2,1,0:T(4,128)} %bitcast.9), channel_id=1, replica_groups=mesh['corpus'=16,'batch'=2] {'corpus'}, dimensions={0} | all-to-all | bytes 65536 | tf_op jit(solution)/shard_map/all_to_all | solution.py:165
  52.0 0.0 copy-start.1
  52.0 0.7 %slice_multiply_fusion = f32[4,16]{1,0:T(4,128)} fusion(f32[4,128]{1,0:T(4,128)S(1)} %reduce_sum.9), kind=kLoop, calls=%fused_computation | loop fusion | flops 64 | bytes 512 | tf_op jit(solution)/shard_map/mul | solution.py:167
  52.6 0.0 copy-done.1
  (1 shorter events, 0.0 us)
Async XLA Ops:
  3.5 19.7 %all-to-all-start = ((f32[16,40,128]{2,1,0:T(8,128)}), f32[16,40,128]{2,1,0:T(8,128)S(1)}, u32[]{:S(2)}, u32[]{:S(2)}) async-start(f32[16,40,128]{2,1,0:T(8,128)} %bitcast.7), calls=%async_computation | async-start | bytes 655360 | tf_op jit(solution)/shard_map/all_to_all | solution.py:139
  23.2 0.7 %copy-start = (f32[16,40,128]{2,1,0:T(8,128)}, f32[16,40,128]{2,1,0:T(8,128)S(1)}, u32[]{:S(2)}) copy-start(f32[16,40,128]{2,1,0:T(8,128)S(1)} %all-to-all-done) | copy-start | bytes 983044
  52.0 0.7 %copy-start.1 = (f32[4,128]{1,0:T(4,128)}, f32[4,128]{1,0:T(4,128)S(1)}, u32[]{:S(2)}) copy-start(f32[4,128]{1,0:T(4,128)S(1)} %reduce_sum.9) | copy-start | bytes 6148

commit v2 on v1

v2 whole, which is shorter than its diff:
```python
import functools

import jax
import jax.numpy as jnp
from jax import lax
from jax.experimental import pallas as pl
from jax.experimental.pallas import tpu as pltpu
from jax.sharding import PartitionSpec as P

LANES = 128
TILE = 256
F32, BF16, I32, I16, F8 = jnp.float32, jnp.bfloat16, jnp.int32, jnp.int16, jnp.float8_e4m3fn
VMEM = pl.BlockSpec(memory_space=pltpu.VMEM)
SMEM = pl.BlockSpec(memory_space=pltpu.SMEM)
HBM = pl.BlockSpec(memory_space=pltpu.HBM)


def near(x):
    return pltpu.with_memory_space_constraint(x, pltpu.VMEM)


def far(x):
    return pltpu.with_memory_space_constraint(x, pltpu.HBM)


def pack_kernel(peers, q_ref, cand_ref, len_ref, out_ref):
    own, width = q_ref.shape
    slots = cand_ref.shape[1]
    vregs = width // LANES
    rows = out_ref.shape[0] // peers
    slot = lax.broadcasted_iota(I32, (1, slots), 1)
    parts = [q_ref[i : i + 1, v * LANES : (v + 1) * LANES] for i in range(own) for v in range(vregs)]
    for i in range(own):
        live = jnp.where(slot < len_ref[i], cand_ref[i : i + 1, :], -1).astype(F32)
        parts.append(jnp.concatenate([live, jnp.full((1, LANES - slots), -1.0, F32)], axis=1))
    fill = rows - own * vregs - own
    if fill:
        parts.append(jnp.zeros((fill, LANES), F32))
    block = jnp.concatenate(parts, axis=0)
    for p in range(peers):
        out_ref[p * rows : (p + 1) * rows, :] = block


def unpack(word):
    blocks = []
    for h in range(2):
        half = lax.shift_right_logical(word, 16 * h).astype(I16)
        planes = []
        for k in range(16):
            bit = jnp.int16(-(2**15) if k == 15 else 1 << k)
            planes.append(jnp.where((half & bit) != 0, BF16(1), BF16(-1)))
        blocks.append(jnp.concatenate(planes, axis=0).astype(F8))
    return blocks


def main_kernel(peers, own, cols, edges_ref, x_ref, codes_hbm, quant_hbm, scale_hbm, out_ref, codes_ref, quant_ref, scale_ref, signs_s, qhl_s, bits_s, place_s, sems):
    first = [
        pltpu.make_async_copy(codes_hbm, codes_ref, sems.at[0]),
        pltpu.make_async_copy(scale_hbm, scale_ref, sems.at[1]),
    ]
    stream = []
    for i in range(quant_hbm.shape[0] // cols):
        at = pl.ds(i * cols, cols)
        stream.append(pltpu.make_async_copy(quant_hbm.at[at, :], quant_ref.at[at, :], sems.at[2 + i]))
    for copy in first + stream:
        copy.start()
    nq = peers * own
    count, width = quant_ref.shape
    vregs = width // LANES
    rows = x_ref.shape[0] // peers
    nedges = edges_ref.shape[0]
    nbins = nedges - 1
    full, index = [], []
    for i in range(own):
        full.append(
            jnp.concatenate([x_ref[pl.ds(i * vregs + v, peers, stride=rows), :] for v in range(vregs)], axis=1)
        )
        index.append(x_ref[pl.ds(own * vregs + i, peers, stride=rows), :].astype(I32))
    full = jnp.concatenate(full, axis=0)
    index = jnp.concatenate(index, axis=0)
    index = jnp.where(index < 0, -1, index - lax.axis_index("corpus") * count)
    low = index & (LANES - 1)
    high = index >> 7
    hi = full.astype(BF16)
    qhl_s[:nq, :] = hi
    qhl_s[nq:, :] = (full - hi.astype(F32)).astype(BF16)
    signs = jnp.where(full >= 0, -0.5, 0.5).astype(BF16)
    src = lax.broadcasted_iota(I32, (2 * TILE, TILE), 0)
    dst = lax.broadcasted_iota(I32, (2 * TILE, TILE), 1)
    for h in range(2):
        perm = jnp.where(src == (dst & 15) * 32 + 16 * h + (dst >> 4), 1.0, 0.0).astype(BF16)
        for b in range(width // (2 * TILE)):
            at = (2 * b + h) * TILE
            signs_s[:, at : at + TILE] = jnp.dot(
                signs[:, 2 * b * TILE : (2 * b + 2) * TILE], perm, preferred_element_type=F32
            ).astype(F8)
    lane = lax.broadcasted_iota(I32, (LANES, LANES), 1)
    for k in range(nbins):
        place_s[k * LANES : (k + 1) * LANES, :] = jnp.where(lane == LANES // 2 + k, 1.0, 0.0).astype(BF16)

    floor = edges_ref[0] - 1
    dist = lax.broadcasted_iota(I32, (8, LANES), 1) + floor
    tables = []
    for j in range(-(-nbins // 4)):
        word = jnp.zeros((8, LANES), I32)
        for k in range(4 * j, min(4 * j + 4, nbins)):
            inside = (dist >= edges_ref[k]) & (dist < edges_ref[k + 1])
            word = word + jnp.where(inside, jnp.int32(1 << (8 * (k - 4 * j))), 0)
        tables.append(jnp.concatenate([word] * (nq // 8), axis=0))
    offset = (width // 2 - floor).astype(F32)
    tally = [jnp.zeros((nq, LANES), I32) for _ in tables]
    scores = jnp.zeros((nq, LANES), F32)
    for copy in first:
        copy.wait()
    for i in range(count // cols):
        at = slice(i * cols, (i + 1) * cols)
        for b in range(width // (2 * TILE)):
            for h, block in enumerate(unpack(codes_ref[16 * b : 16 * b + 16, at])):
                bits_s[(2 * b + h) * TILE : (2 * b + h + 1) * TILE, at] = block
        half = jnp.dot(signs_s[...], bits_s[:, at], preferred_element_type=F32)
        stream[i].wait()
        prod = lax.dot_general(
            qhl_s[...], quant_ref[at, :], (((1,), (1,)), ((), ())), preferred_element_type=F32
        )
        for j in range(cols // LANES):
            cut = slice(j * LANES, (j + 1) * LANES)
            where = jnp.clip(half[:, cut] + offset, 0.0, LANES - 1.0).astype(I32)
            tally = [
                t + jnp.take_along_axis(w, where, axis=1, mode="promise_in_bounds") for t, w in zip(tally, tables)
            ]
            row = i * (cols // LANES) + j
            value = (prod[:nq, cut] + prod[nq:, cut]) * scale_ref[:, row * LANES : (row + 1) * LANES]
            value = jnp.take_along_axis(value, low, axis=1, mode="promise_in_bounds")
            scores = jnp.where(high == row, value, scores)
    planes = []
    for k in range(nbins):
        planes.append(((tally[k // 4] >> (8 * (k % 4))) & 255).astype(F32).astype(BF16))
    counts = jnp.dot(jnp.concatenate(planes, axis=1), place_s[...], preferred_element_type=F32)
    lane = lax.broadcasted_iota(I32, (nq, LANES), 1)
    res = jnp.where(lane < LANES // 2, scores, counts)
    for i in range(own):
        out_ref[pl.ds(i, peers, stride=own), :] = res[i * peers : (i + 1) * peers, :]


def shards(peers, queries, codes, quant_rows, row_scale, candidates, shortlist, edges):
    own, width = queries.shape
    slots = candidates.shape[1]
    count, words = codes.shape
    nbins = edges.shape[0] - 1
    nq = own * peers
    rows = -(-(own * (width // LANES) + own) // 8) * 8
    assert words % 16 == 0 and width == 32 * words and count % 512 == 0
    assert count // LANES < 256 and slots <= LANES // 2 and nbins <= LANES // 2
    payload = pl.pallas_call(
        functools.partial(pack_kernel, peers),
        in_specs=[VMEM, VMEM, SMEM],
        out_specs=VMEM,
        out_shape=pltpu.VMEM((peers * rows, LANES), F32),
        name="pack",
    )(far(queries), far(candidates), far(shortlist))
    got = lax.all_to_all(payload, "corpus", 0, 0, tiled=True)
    part = pl.pallas_call(
        functools.partial(main_kernel, peers, own, 512),
        in_specs=[SMEM, VMEM, HBM, HBM, HBM],
        out_specs=VMEM,
        out_shape=pltpu.VMEM((nq, LANES), F32),
        scratch_shapes=[
            pltpu.VMEM((words, count), I32),
            pltpu.VMEM((count, width), BF16),
            pltpu.VMEM((1, count), F32),
            pltpu.VMEM((nq, width), F8),
            pltpu.VMEM((2 * nq, width), BF16),
            pltpu.VMEM((width, count), F8),
            pltpu.VMEM((nbins * LANES, LANES), BF16),
            pltpu.SemaphoreType.DMA((2 + count // 512,)),
        ],
        compiler_params=pltpu.CompilerParams(vmem_limit_bytes=48 << 20),
        cost_estimate=pl.CostEstimate(flops=4 * 10**9, bytes_accessed=0, transcendentals=0),
        name="main",
    )(far(edges), near(got), far(codes.T), far(quant_rows), far(row_scale.reshape(1, count)))
    back = lax.all_to_all(part, "corpus", 0, 0, tiled=True)
    total = jnp.sum(back.reshape(peers, own, LANES), axis=0)
    hist = total[:, LANES // 2 : LANES // 2 + nbins] * (nbins / (count * peers))
    return hist, total[:, :slots]


def solution(mesh):
    both = ("corpus", "batch")
    return jax.shard_map(
        functools.partial(shards, mesh.shape["corpus"]),
        mesh=mesh,
        in_specs=(P(both, None), P("corpus", None), P("corpus", None), P("corpus"), P(both, None), P(both), P()),
        out_specs=(P(both, None), P(both, None)),
        check_vma=False,
    )
```

time: 53 us -> 42.6 us (0.80)
  blocking collectives: 10.9 us -> 30.2 us
  starting transfers between devices: 8.34 us -> 0 us
  waiting for transfers between devices: 8.18 us -> 0 us
  Pallas kernels: 18.7 us -> 10.7 us
  local copies, waits for them, and re-layouts: 5.18 us -> 0.01 us
    all_to_all x0 -> x1, blocking collectives: none -> 19.5 us  [shards(): got = lax.all_to_all(payload, 'corpus', 0, 0, tiled=True)]
    all_to_all x1 -> x0, starting transfers between devices: 8.34 us -> none  [shards(): got = lax.all_to_all(payload, 'corpus', 0, 0, tiled=True)]
    all_to_all x1 -> x0, waiting for transfers between devices: 8.18 us -> none  [shards(): got = lax.all_to_all(payload, 'corpus', 0, 0, tiled=True)]
    pallas_call x2, Pallas kernels: 18.7 us -> 10.7 us  [the longest x1 9.92 us: shards(): pl.pallas_call(functools.partial(main_kernel, peers, own, 512), in_specs=...]
    unnamed x5 -> x2, local copies, waits for them, and re-layouts: 3.87 us -> 0.01 us
    reshape x1 -> x0, local copies, waits for them, and re-layouts: 1.31 us -> none  [shards(): shortlist.reshape(own, 1)]
  transfers between devices with their start and end apart: 1 -> 0, of which waited for: 1 -> 0; matrix products, arithmetic and copies ran while one was open for 6% -> 0% of each run, Pallas kernels for 0% -> 0%
where the time goes in v2:
time: 42.6 us; the launch traced here: 42.2 us
  blocking collectives  30.2 us (71%)
  Pallas kernels  10.7 us (25%)
  other arithmetic  0.68 us (2%)
  between operations  0.65 us (2%)
    all_to_all x1, blocking collectives, shards(): got = lax.all_to_all(payload, 'corpus', 0, 0, tiled=True)  19.5 us
    all_to_all x1, blocking collectives, shards(): back = lax.all_to_all(part, 'corpus', 0, 0, tiled=True)  10.7 us
    pallas_call x1, Pallas kernels, shards(): pl.pallas_call(functools.partial(main_kernel, peers, own, 512), in_specs=...  9.92 us

profile of v2, /device:TPU:0, one launch (start us, length us, event | category | flops | bytes accessed | tf_op | source)
XLA Modules:
  0.0 42.2 jit_solution(10371429417019235550)
XLA Ops:
  0.6 0.8 %pack.1 = f32[640,128]{1,0:T(8,128)S(1)} custom-call(f32[4,1024]{1,0:T(4,128)} %q_ref.1, s32[4,40]{1,0:T(4,128)} %cand_ref.1, s32[4]{0:T(128)} %len_ref.1), custom_call_target="tpu_custom_call" | custom-call | tf_op jit(solution)/shard_map/pack/pallas_call | solution.py:154
  1.5 19.5 %all_to_all.20 = f32[16,40,128]{2,1,0:T(8,128)S(1)} all-to-all(f32[16,40,128]{2,1,0:T(8,128)S(1)} %bitcast.6), channel_id=1, replica_groups=mesh['corpus'=16,'batch'=2] {'corpus'}, dimensions={0} | all-to-all | bytes 655360 | tf_op jit(solution)/shard_map/all_to_all | solution.py:161
  20.9 9.9 %main.1 = f32[64,128]{1,0:T(8,128)S(1)} custom-call(s32[17]{0:T(128)} %edges_ref.1, f32[640,128]{1,0:T(8,128)S(1)} %bitcast.7, s32[32,6144]{1,0:T(8,128)} %bitcast.10, bf16[6144,1024]{1,0:T(8,128)(2,1)} %quant_hbm.1, f32[1,6144]{1,0:T(1,128)} %bitcast.11), custom_call_target="tpu_custom_call" | custom-call | flops 4000000000 | tf_op jit(solution)/shard_map/main/pallas_call | solution.py:162
  30.8 10.7 %all_to_all.21 = f32[16,4,128]{2,1,0:T(4,128)S(1)} all-to-all(f32[16,4,128]{2,1,0:T(4,128)S(1)} %bitcast.8), channel_id=1, replica_groups=mesh['corpus'=16,'batch'=2] {'corpus'}, dimensions={0} | all-to-all | bytes 65536 | tf_op jit(solution)/shard_map/all_to_all | solution.py:181
  41.6 0.0 copy-start
  41.6 0.7 %slice_multiply_fusion = f32[4,16]{1,0:T(4,128)} fusion(f32[4,128]{1,0:T(4,128)S(1)} %reduce_sum.9), kind=kLoop, calls=%fused_computation | loop fusion | flops 64 | bytes 512 | tf_op jit(solution)/shard_map/mul | solution.py:183
  42.2 0.0 copy-done
  (1 shorter events, 0.0 us)
Async XLA Ops:
  41.6 0.7 %copy-start = (f32[4,128]{1,0:T(4,128)}, f32[4,128]{1,0:T(4,128)S(1)}, u32[]{:S(2)}) copy-start(f32[4,128]{1,0:T(4,128)S(1)} %reduce_sum.9) | copy-start | bytes 6148

commit v3 on v2

v3 whole, which is shorter than its diff:
```python
import functools
import math

import jax
import jax.numpy as jnp
from jax import lax
from jax.experimental import pallas as pl
from jax.experimental.pallas import tpu as pltpu
from jax.sharding import PartitionSpec as P

LANES = 128
TILE = 256
F32, BF16, I32, I16, F8 = jnp.float32, jnp.bfloat16, jnp.int32, jnp.int16, jnp.float8_e4m3fn
VMEM = pl.BlockSpec(memory_space=pltpu.VMEM)
SMEM = pl.BlockSpec(memory_space=pltpu.SMEM)
ANY = pl.BlockSpec(memory_space=pl.ANY)


def near(x):
    return pltpu.with_memory_space_constraint(x, pltpu.VMEM)


def far(x):
    return pltpu.with_memory_space_constraint(x, pltpu.HBM)


def pack_kernel(peers, q_hbm, cand_hbm, len_hbm, edges_hbm, out_ref, table_ref, q_ref, cand_ref, len_ref, edges_ref, sems):
    pairs = [(q_hbm, q_ref), (cand_hbm, cand_ref), (len_hbm, len_ref), (edges_hbm, edges_ref)]
    moves = [pltpu.make_async_copy(*pair, sems.at[n]) for n, pair in enumerate(pairs)]
    for move in moves:
        move.start()
    for move in moves:
        move.wait()
    own, width = q_ref.shape
    slots = cand_ref.shape[1]
    rows = out_ref.shape[0] // peers
    slot = lax.broadcasted_iota(I32, (1, slots), 1)
    dead = jnp.full((1, LANES // 2 - slots), -1.0, F32)
    parts = [q_ref[i : i + 1, v * LANES : (v + 1) * LANES] for i in range(own) for v in range(width // LANES)]
    lists = []
    for i in range(own):
        lists += [jnp.where(slot < len_ref[i], cand_ref[i : i + 1, :], -1).astype(F32), dead]
    for i in range(0, own, 2):
        parts.append(jnp.concatenate(lists[2 * i : 2 * i + 4], axis=1))
    block = jnp.concatenate(parts, axis=0)
    for p in range(peers):
        out_ref[p * rows : (p + 1) * rows, :] = block
    nbins = edges_ref.shape[0] - 1
    floor = edges_ref[0] - 1
    dist = lax.broadcasted_iota(I32, (8, LANES), 1) + floor
    for j in range(-(-nbins // 4)):
        word = jnp.zeros((8, LANES), I32)
        for k in range(4 * j, min(4 * j + 4, nbins)):
            inside = (dist >= edges_ref[k]) & (dist < edges_ref[k + 1])
            word = word + jnp.where(inside, jnp.int32(1 << (8 * (k - 4 * j))), 0)
        table_ref[8 * j : 8 * j + 8, :] = word
    table_ref[-8:, :] = jnp.full((8, LANES), width // 2 - floor, I32)


def unpack(word):
    blocks = []
    for h in range(2):
        half = lax.shift_right_logical(word, 16 * h).astype(I16)
        planes = []
        for k in range(16):
            bit = jnp.int16(-(2**15) if k == 15 else 1 << k)
            planes.append(jnp.where((half & bit) != 0, BF16(1), BF16(-1)))
        blocks.append(jnp.concatenate(planes, axis=0).astype(F8))
    return blocks


def main_kernel(own, group, cols, nbins, table_ref, x_ref, codes_ref, quant_ref, scale_ref, out_ref, signs_s, qhl_s, bits_s, place_s):
    count, width = quant_ref.shape
    vregs = width // LANES
    rows = own * vregs + -(-own // 2)
    peers = x_ref.shape[0] // rows
    nq = group * own
    src = lax.broadcasted_iota(I32, (2 * TILE, TILE), 0)
    dst = lax.broadcasted_iota(I32, (2 * TILE, TILE), 1)
    perms = [jnp.where(src == (dst & 15) * 32 + 16 * h + (dst >> 4), 1.0, 0.0).astype(BF16) for h in range(2)]
    lane = lax.broadcasted_iota(I32, (LANES, LANES), 1)
    for k in range(nbins):
        place_s[k * LANES : (k + 1) * LANES, :] = jnp.where(lane == LANES // 2 + k, 1.0, 0.0).astype(BF16)
    tables = [
        jnp.concatenate([table_ref[8 * j : 8 * j + 8, :]] * (nq // 8), axis=0) for j in range(table_ref.shape[0] // 8 - 1)
    ]
    offset = jnp.concatenate([table_ref[-8:, :].astype(F32)] * (nq // 8), axis=0)

    def serve(start):
        lane = lax.broadcasted_iota(I32, (group, LANES), 1)
        full, index = [], []
        for i in range(own):
            at = start * rows + i * vregs
            full.append(jnp.concatenate([x_ref[pl.ds(at + v, group, stride=rows), :] for v in range(vregs)], axis=1))
            got = x_ref[pl.ds(start * rows + own * vregs + i // 2, group, stride=rows), :]
            if i % 2:
                got = pltpu.roll(got, LANES // 2, 1)
            index.append(jnp.where(lane < LANES // 2, got, -1.0).astype(I32))
        full = jnp.concatenate(full, axis=0)
        index = jnp.concatenate(index, axis=0)
        index = jnp.where(index < 0, -1, index - lax.axis_index("corpus") * count)
        low = index & (LANES - 1)
        high = index >> 7
        hi = full.astype(BF16)
        qhl_s[:nq, :] = hi
        qhl_s[nq:, :] = (full - hi.astype(F32)).astype(BF16)
        signs = jnp.where(full >= 0, -0.5, 0.5).astype(BF16)
        for h in range(2):
            for b in range(width // (2 * TILE)):
                at = (2 * b + h) * TILE
                signs_s[:, at : at + TILE] = jnp.dot(
                    signs[:, 2 * b * TILE : (2 * b + 2) * TILE], perms[h], preferred_element_type=F32
                ).astype(F8)

        tally = [jnp.zeros((nq, LANES), I32) for _ in tables]
        scores = jnp.zeros((nq, LANES), F32)
        for i in range(count // cols):
            at = slice(i * cols, (i + 1) * cols)
            for b in range(width // (2 * TILE)):
                for h, block in enumerate(unpack(codes_ref[16 * b : 16 * b + 16, at])):
                    bits_s[(2 * b + h) * TILE : (2 * b + h + 1) * TILE, at] = block
            half = jnp.dot(signs_s[...], bits_s[:, at], preferred_element_type=F32)
            prod = lax.dot_general(
                qhl_s[...], quant_ref[at, :], (((1,), (1,)), ((), ())), preferred_element_type=F32
            )
            for j in range(cols // LANES):
                cut = slice(j * LANES, (j + 1) * LANES)
                where = jnp.clip(half[:, cut] + offset, 0.0, LANES - 1.0).astype(I32)
                tally = [
                    t + jnp.take_along_axis(w, where, axis=1, mode="promise_in_bounds") for t, w in zip(tally, tables)
                ]
                row = i * (cols // LANES) + j
                value = (prod[:nq, cut] + prod[nq:, cut]) * scale_ref[:, row * LANES : (row + 1) * LANES]
                value = jnp.take_along_axis(value, low, axis=1, mode="promise_in_bounds")
                scores = jnp.where(high == row, value, scores)
        planes = [((tally[k // 4] >> (8 * (k % 4))) & 255).astype(F32).astype(BF16) for k in range(nbins)]
        counts = jnp.dot(jnp.concatenate(planes, axis=1), place_s[...], preferred_element_type=F32)
        lane = lax.broadcasted_iota(I32, (nq, LANES), 1)
        res = jnp.where(lane < LANES // 2, scores, counts)
        for i in range(own):
            out_ref[pl.ds(start * own + i, group, stride=own), :] = res[i * group : (i + 1) * group, :]

    if peers == group:
        serve(0)
    else:
        pl.loop(0, peers // group)(lambda g: serve(g * group))


def shards(peers, queries, codes, quant_rows, row_scale, candidates, shortlist, edges):
    own, width = queries.shape
    slots = candidates.shape[1]
    count, words = codes.shape
    nbins = edges.shape[0] - 1
    nq = own * peers
    cols = 768 if count % 768 == 0 else 512
    group = math.gcd(peers, 16)
    part = group * own
    rows = own * (width // LANES) + -(-own // 2)
    assert words % 16 == 0 and width == 32 * words and count % 512 == 0
    assert count // LANES < 256 and slots <= LANES // 2 and nbins <= LANES // 2
    payload, table = pl.pallas_call(
        functools.partial(pack_kernel, peers),
        in_specs=[ANY, ANY, ANY, ANY],
        out_specs=[VMEM, VMEM],
        out_shape=[
            pltpu.VMEM((peers * rows, LANES), F32),
            pltpu.VMEM((8 * -(-nbins // 4) + 8, LANES), I32),
        ],
        scratch_shapes=[
            pltpu.VMEM(queries.shape, F32),
            pltpu.VMEM(candidates.shape, I32),
            pltpu.SMEM(shortlist.shape, I32),
            pltpu.SMEM(edges.shape, I32),
            pltpu.SemaphoreType.DMA((4,)),
        ],
        compiler_params=pltpu.CompilerParams(vmem_limit_bytes=2 << 20),
        cost_estimate=pl.CostEstimate(flops=10**10, bytes_accessed=0, transcendentals=0),
        name="pack",
    )(far(queries), far(candidates), far(shortlist), far(edges))
    got = lax.all_to_all(payload.reshape(peers, 1, rows * LANES), "corpus", 0, 0)
    got = got.reshape(peers * rows, LANES)
    result = pl.pallas_call(
        functools.partial(main_kernel, own, group, cols, nbins),
        in_specs=[VMEM, VMEM, VMEM, VMEM, VMEM],
        out_specs=VMEM,
        out_shape=pltpu.VMEM((nq, LANES), F32),
        scratch_shapes=[
            pltpu.VMEM((part, width), F8),
            pltpu.VMEM((2 * part, width), BF16),
            pltpu.VMEM((width, count), F8),
            pltpu.VMEM((nbins * LANES, LANES), BF16),
        ],
        compiler_params=pltpu.CompilerParams(vmem_limit_bytes=24 << 20),
        cost_estimate=pl.CostEstimate(flops=4 * 10**9, bytes_accessed=0, transcendentals=0),
        name="main",
    )(near(table), near(got), codes.T, quant_rows, row_scale.reshape(1, count))
    back = lax.all_to_all(result, "corpus", 0, 0, tiled=True)
    total = jnp.sum(back.reshape(peers, own, LANES), axis=0)
    hist = total[:, LANES // 2 : LANES // 2 + nbins] * (nbins / (count * peers))
    return hist, total[:, :slots]


def solution(mesh):
    both = ("corpus", "batch")
    return jax.shard_map(
        functools.partial(shards, mesh.shape["corpus"]),
        mesh=mesh,
        in_specs=(P(both, None), P("corpus", None), P("corpus", None), P("corpus"), P(both, None), P(both), P()),
        out_specs=(P(both, None), P(both, None)),
        check_vma=False,
    )
```

time: 42.6 us -> 37.1 us (0.87)
  Pallas kernels: 10.7 us -> 6.17 us
  blocking collectives: 30.2 us -> 29.4 us
    pallas_call x2, Pallas kernels: 10.7 us -> 6.17 us  [the longest x1 5.16 us: shards(): pl.pallas_call(functools.partial(main_kernel, own, group, cols, nbins), i...]
    all_to_all x2, blocking collectives: 30.2 us -> 29.4 us  [the longest x1 18.8 us: shards(): lax.all_to_all(payload.reshape(peers, 1, rows * LANES), 'corpus', 0, 0)]
where the time goes in v3:
time: 37.1 us; the launch traced here: 36.9 us
  blocking collectives  29.4 us (79%)
  Pallas kernels  6.17 us (17%)
  other arithmetic  0.68 us (2%)
  between operations  0.67 us (2%)
    all_to_all x1, blocking collectives, shards(): lax.all_to_all(payload.reshape(peers, 1, rows * LANES), 'corpus', 0, 0)  18.8 us
    all_to_all x1, blocking collectives, shards(): back = lax.all_to_all(result, 'corpus', 0, 0, tiled=True)  10.6 us
    pallas_call x1, Pallas kernels, shards(): pl.pallas_call(functools.partial(main_kernel, own, group, cols, nbins), i...  5.16 us
    pallas_call x1, Pallas kernels, shards(): pl.pallas_call(functools.partial(pack_kernel, peers), in_specs=[ANY, ANY,...  1 us

profile of v3, /device:TPU:0, one launch (start us, length us, event | category | flops | bytes accessed | tf_op | source)
XLA Modules:
  0.0 36.9 jit_solution(16793240819456018276)
XLA Ops:
  0.6 0.0 copy-start.2
  0.6 0.0 copy-start
  0.7 0.0 copy-start.1
  0.7 1.0 %pack.1 = (f32[544,128]{1,0:T(8,128)S(1)}, s32[40,128]{1,0:T(8,128)S(1)}) custom-call(f32[4,1024]{1,0:T(4,128)} %q_hbm.1, s32[4,40]{1,0:T(4,128)} %cand_hbm.1, s32[4]{0:T(128)} %len_hbm.1, s32[17]{0:T(128)} %edges_hbm.1), custom_call_target="tpu_custom_call" | custom-call | flops 10000000000 | tf_op jit(solution)/shard_map/pack/pallas_call | solution.py:161
  1.7 18.8 %all_to_all.14 = f32[16,1,4352]{2,1,0:T(1,128)S(1)} all-to-all(f32[16,1,4352]{2,1,0:T(1,128)S(1)} %bitcast.7), channel_id=1, replica_groups=mesh['corpus'=16,'batch'=2] {'corpus'}, dimensions={0} | all-to-all | bytes 557056 | tf_op jit(solution)/shard_map/all_to_all | solution.py:180
  20.4 0.0 copy-done.2
  20.4 0.0 copy-done
  20.4 0.0 copy-done.1
  20.5 5.2 %main.1 = f32[64,128]{1,0:T(8,128)S(1)} custom-call(s32[40,128]{1,0:T(8,128)S(1)} %get-tuple-element.4.table_ref, f32[544,128]{1,0:T(8,128)S(1)} %bitcast.6, s32[32,6144]{1,0:T(8,128)S(1)} %bitcast.9, bf16[6144,1024]{1,0:T(8,128)(2,1)S(1)} %copy-done, f32[1,6144]{1,0:T(1,128)S(1)} %bitcast.10), custom_call_target="tpu_custom_call" | custom-call | flops 4000000000 | tf_op jit(solution)/shard_map/main/pallas_call | solution.py:182
  25.6 10.6 %all_to_all.15 = f32[16,4,128]{2,1,0:T(4,128)S(1)} all-to-all(f32[16,4,128]{2,1,0:T(4,128)S(1)} %bitcast.8), channel_id=1, replica_groups=mesh['corpus'=16,'batch'=2] {'corpus'}, dimensions={0} | all-to-all | bytes 65536 | tf_op jit(solution)/shard_map/all_to_all | solution.py:197
  36.2 0.0 copy-start.3
  36.3 0.7 %slice_multiply_fusion = f32[4,16]{1,0:T(4,128)} fusion(f32[4,128]{1,0:T(4,128)S(1)} %reduce_sum.9), kind=kLoop, calls=%fused_computation | loop fusion | flops 64 | bytes 512 | tf_op jit(solution)/shard_map/mul | solution.py:199
  36.9 0.0 copy-done.3
  (1 shorter events, 0.0 us)
Async XLA Ops:
  0.6 19.8 %copy-start.2 = (f32[6144]{0:T(1024)S(1)}, f32[6144]{0:T(1024)}, u32[]{:S(2)}) copy-start(f32[6144]{0:T(1024)} %param.10) | copy-start | bytes 73732
  0.6 19.8 %copy-start = (bf16[6144,1024]{1,0:T(8,128)(2,1)S(1)}, bf16[6144,1024]{1,0:T(8,128)(2,1)}, u32[]{:S(2)}) copy-start(bf16[6144,1024]{1,0:T(8,128)(2,1)} %quant_ref.1) | copy-start | bytes 37748740
  0.7 19.8 %copy-start.1 = (s32[6144,32]{0,1:T(8,128)S(1)}, s32[6144,32]{0,1:T(8,128)}, u32[]{:S(2)}) copy-start(s32[6144,32]{0,1:T(8,128)} %param.8) | copy-start | bytes 2359300
  36.2 0.7 %copy-start.3 = (f32[4,128]{1,0:T(4,128)}, f32[4,128]{1,0:T(4,128)S(1)}, u32[]{:S(2)}) copy-start(f32[4,128]{1,0:T(4,128)S(1)} %reduce_sum.9) | copy-start | bytes 6148

commit v4 on v3

--- a/solution.py
+++ b/solution.py
@@ -24,7 +24,7 @@
     return pltpu.with_memory_space_constraint(x, pltpu.HBM)
 
 
-def pack_kernel(peers, q_hbm, cand_hbm, len_hbm, edges_hbm, out_ref, table_ref, q_ref, cand_ref, len_ref, edges_ref, sems):
+def pack_kernel(share, q_hbm, cand_hbm, len_hbm, edges_hbm, out_ref, table_ref, q_ref, cand_ref, len_ref, edges_ref, sems):
     pairs = [(q_hbm, q_ref), (cand_hbm, cand_ref), (len_hbm, len_ref), (edges_hbm, edges_ref)]
     moves = [pltpu.make_async_copy(*pair, sems.at[n]) for n, pair in enumerate(pairs)]
     for move in moves:
@@ -33,17 +33,19 @@
         move.wait()
     own, width = q_ref.shape
     slots = cand_ref.shape[1]
-    rows = out_ref.shape[0] // peers
     slot = lax.broadcasted_iota(I32, (1, slots), 1)
     dead = jnp.full((1, LANES // 2 - slots), -1.0, F32)
-    parts = [q_ref[i : i + 1, v * LANES : (v + 1) * LANES] for i in range(own) for v in range(width // LANES)]
-    lists = []
-    for i in range(own):
-        lists += [jnp.where(slot < len_ref[i], cand_ref[i : i + 1, :], -1).astype(F32), dead]
-    for i in range(0, own, 2):
-        parts.append(jnp.concatenate(lists[2 * i : 2 * i + 4], axis=1))
+    parts = []
+    for first in range(0, own, share):
+        lists = []
+        for i in range(first, first + share):
+            parts += [q_ref[i : i + 1, v * LANES : (v + 1) * LANES] for v in range(width // LANES)]
+            lists += [jnp.where(slot < len_ref[i], cand_ref[i : i + 1, :], -1).astype(F32), dead]
+        for i in range(0, share, 2):
+            parts.append(jnp.concatenate(lists[2 * i : 2 * i + 4], axis=1))
     block = jnp.concatenate(parts, axis=0)
-    for p in range(peers):
+    rows = block.shape[0]
+    for p in range(out_ref.shape[0] // rows):
         out_ref[p * rows : (p + 1) * rows, :] = block
     nbins = edges_ref.shape[0] - 1
     floor = edges_ref[0] - 1
@@ -69,12 +71,12 @@
     return blocks
 
 
-def main_kernel(own, group, cols, nbins, table_ref, x_ref, codes_ref, quant_ref, scale_ref, out_ref, signs_s, qhl_s, bits_s, place_s):
+def main_kernel(share, group, cols, nbins, table_ref, x_ref, codes_ref, quant_ref, scale_ref, out_ref, signs_s, qhl_s, bits_s, place_s):
     count, width = quant_ref.shape
     vregs = width // LANES
-    rows = own * vregs + -(-own // 2)
-    peers = x_ref.shape[0] // rows
-    nq = group * own
+    rows = share * vregs + share // 2
+    sources = x_ref.shape[0] // rows
+    nq = group * share
     src = lax.broadcasted_iota(I32, (2 * TILE, TILE), 0)
     dst = lax.broadcasted_iota(I32, (2 * TILE, TILE), 1)
     perms = [jnp.where(src == (dst & 15) * 32 + 16 * h + (dst >> 4), 1.0, 0.0).astype(BF16) for h in range(2)]
@@ -89,10 +91,10 @@
     def serve(start):
         lane = lax.broadcasted_iota(I32, (group, LANES), 1)
         full, index = [], []
-        for i in range(own):
+        for i in range(share):
             at = start * rows + i * vregs
             full.append(jnp.concatenate([x_ref[pl.ds(at + v, group, stride=rows), :] for v in range(vregs)], axis=1))
-            got = x_ref[pl.ds(start * rows + own * vregs + i // 2, group, stride=rows), :]
+            got = x_ref[pl.ds(start * rows + share * vregs + i // 2, group, stride=rows), :]
             if i % 2:
                 got = pltpu.roll(got, LANES // 2, 1)
             index.append(jnp.where(lane < LANES // 2, got, -1.0).astype(I32))
@@ -137,33 +139,37 @@
         counts = jnp.dot(jnp.concatenate(planes, axis=1), place_s[...], preferred_element_type=F32)
         lane = lax.broadcasted_iota(I32, (nq, LANES), 1)
         res = jnp.where(lane < LANES // 2, scores, counts)
-        for i in range(own):
-            out_ref[pl.ds(start * own + i, group, stride=own), :] = res[i * group : (i + 1) * group, :]
-
-    if peers == group:
+        for i in range(share):
+            out_ref[pl.ds(start * share + i, group, stride=share), :] = res[i * group : (i + 1) * group, :]
+
+    if sources == group:
         serve(0)
     else:
-        pl.loop(0, peers // group)(lambda g: serve(g * group))
-
-
-def shards(peers, queries, codes, quant_rows, row_scale, candidates, shortlist, edges):
+        pl.loop(0, sources // group)(lambda g: serve(g * group))
+
+
+def shards(chips, cores, queries, codes, quant_rows, row_scale, candidates, shortlist, edges):
+    both = ("corpus", "batch")
     own, width = queries.shape
     slots = candidates.shape[1]
     count, words = codes.shape
     nbins = edges.shape[0] - 1
-    nq = own * peers
+    devices = chips * cores
+    share = own // cores
+    nq = share * devices
     cols = 768 if count % 768 == 0 else 512
-    group = math.gcd(peers, 16)
-    part = group * own
-    rows = own * (width // LANES) + -(-own // 2)
+    group = math.gcd(devices, 32)
+    part = group * share
+    rows = share * (width // LANES) + share // 2
+    assert own % (2 * cores) == 0
     assert words % 16 == 0 and width == 32 * words and count % 512 == 0
     assert count // LANES < 256 and slots <= LANES // 2 and nbins <= LANES // 2
     payload, table = pl.pallas_call(
-        functools.partial(pack_kernel, peers),
+        functools.partial(pack_kernel, share),
         in_specs=[ANY, ANY, ANY, ANY],
         out_specs=[VMEM, VMEM],
         out_shape=[
-            pltpu.VMEM((peers * rows, LANES), F32),
+            pltpu.VMEM((devices * rows, LANES), F32),
             pltpu.VMEM((8 * -(-nbins // 4) + 8, LANES), I32),
         ],
         scratch_shapes=[
@@ -177,10 +183,9 @@
         cost_estimate=pl.CostEstimate(flops=10**10, bytes_accessed=0, transcendentals=0),
         name="pack",
     )(far(queries), far(candidates), far(shortlist), far(edges))
-    got = lax.all_to_all(payload.reshape(peers, 1, rows * LANES), "corpus", 0, 0)
-    got = got.reshape(peers * rows, LANES)
+    got = lax.all_to_all(payload.reshape(devices, 1, rows * LANES), both, 0, 0).reshape(devices * rows, LANES)
     result = pl.pallas_call(
-        functools.partial(main_kernel, own, group, cols, nbins),
+        functools.partial(main_kernel, share, group, cols, nbins),
         in_specs=[VMEM, VMEM, VMEM, VMEM, VMEM],
         out_specs=VMEM,
         out_shape=pltpu.VMEM((nq, LANES), F32),
@@ -194,16 +199,16 @@
         cost_estimate=pl.CostEstimate(flops=4 * 10**9, bytes_accessed=0, transcendentals=0),
         name="main",
     )(near(table), near(got), codes.T, quant_rows, row_scale.reshape(1, count))
-    back = lax.all_to_all(result, "corpus", 0, 0, tiled=True)
-    total = jnp.sum(back.reshape(peers, own, LANES), axis=0)
-    hist = total[:, LANES // 2 : LANES // 2 + nbins] * (nbins / (count * peers))
+    back = lax.all_to_all(result.reshape(devices, 1, share * LANES), both, 0, 0)
+    total = jnp.sum(back.reshape(chips, own, LANES), axis=0)
+    hist = total[:, LANES // 2 : LANES // 2 + nbins] * (nbins / (count * chips))
     return hist, total[:, :slots]
 
 
 def solution(mesh):
     both = ("corpus", "batch")
     return jax.shard_map(
-        functools.partial(shards, mesh.shape["corpus"]),
+        functools.partial(shards, mesh.shape["corpus"], mesh.shape["batch"]),
         mesh=mesh,
         in_specs=(P(both, None), P("corpus", None), P("corpus", None), P("corpus"), P(both, None), P(both), P()),
         out_specs=(P(both, None), P(both, None)),

time: 37.1 us -> 35.3 us (0.951)
  blocking collectives: 29.4 us -> 27.5 us
    all_to_all x2, blocking collectives: 29.4 us -> 27.5 us  [the longest x1 18.2 us: shards(): lax.all_to_all(payload.reshape(devices, 1, rows * LANES), both, 0, 0)]
where the time goes in v4:
time: 35.3 us; the launch traced here: 35.1 us
  blocking collectives  27.5 us (78%)
  Pallas kernels  6.19 us (18%)
  other arithmetic  0.68 us (2%)
  between operations  0.68 us (2%)
    all_to_all x1, blocking collectives, shards(): lax.all_to_all(payload.reshape(devices, 1, rows * LANES), both, 0, 0)  18.2 us
    all_to_all x1, blocking collectives, shards(): back = lax.all_to_all(result.reshape(devices, 1, share * LANES), both, 0, 0)  9.31 us
    pallas_call x1, Pallas kernels, shards(): pl.pallas_call(functools.partial(main_kernel, share, group, cols, nbins),...  5.19 us
    pallas_call x1, Pallas kernels, shards(): pl.pallas_call(functools.partial(pack_kernel, share), in_specs=[ANY, ANY,...  1.01 us

profile of v4, /device:TPU:0, one launch (start us, length us, event | category | flops | bytes accessed | tf_op | source)
XLA Modules:
  0.0 35.1 jit_solution(1647085893931442147)
XLA Ops:
  0.6 0.0 copy-start.2
  0.6 0.0 copy-start
  0.7 0.0 copy-start.1
  0.7 1.0 %pack.1 = (f32[544,128]{1,0:T(8,128)S(1)}, s32[40,128]{1,0:T(8,128)S(1)}) custom-call(f32[4,1024]{1,0:T(4,128)} %q_hbm.1, s32[4,40]{1,0:T(4,128)} %cand_hbm.1, s32[4]{0:T(128)} %len_hbm.1, s32[17]{0:T(128)} %edges_hbm.1), custom_call_target="tpu_custom_call" | custom-call | flops 10000000000 | tf_op jit(solution)/shard_map/pack/pallas_call | solution.py:167
  1.7 18.2 %all_to_all.10 = f32[32,1,2176]{2,1,0:T(1,128)S(1)} all-to-all(f32[32,1,2176]{2,1,0:T(1,128)S(1)} %bitcast.8), channel_id=1, replica_groups=mesh['corpus'=16,'batch'=2] {'corpus','batch'}, dimensions={0} | all-to-all | bytes 557056 | tf_op jit(solution)/shard_map/all_to_all | solution.py:186
  19.9 0.0 copy-done.2
  19.9 0.0 copy-done
  19.9 0.0 copy-done.1
  19.9 5.2 %main.1 = f32[64,128]{1,0:T(8,128)S(1)} custom-call(s32[40,128]{1,0:T(8,128)S(1)} %get-tuple-element.4.table_ref, f32[544,128]{1,0:T(8,128)S(1)} %bitcast.7, s32[32,6144]{1,0:T(8,128)S(1)} %bitcast.10, bf16[6144,1024]{1,0:T(8,128)(2,1)S(1)} %copy-done, f32[1,6144]{1,0:T(1,128)S(1)} %bitcast.11), custom_call_target="tpu_custom_call" | custom-call | flops 4000000000 | tf_op jit(solution)/shard_map/main/pallas_call | solution.py:187
  25.1 9.3 %all_to_all.11 = f32[32,1,256]{2,1,0:T(1,128)S(1)} all-to-all(f32[32,1,256]{2,1,0:T(1,128)S(1)} %bitcast.9), channel_id=1, replica_groups=mesh['corpus'=16,'batch'=2] {'corpus','batch'}, dimensions={0} | all-to-all | bytes 65536 | tf_op jit(solution)/shard_map/all_to_all | solution.py:202
  34.4 0.0 copy-start.3
  34.4 0.7 %slice_multiply_fusion = f32[4,16]{1,0:T(4,128)} fusion(f32[4,128]{1,0:T(4,128)S(1)} %reduce_sum.9), kind=kLoop, calls=%fused_computation | loop fusion | flops 64 | bytes 512 | tf_op jit(solution)/shard_map/mul | solution.py:204
  35.1 0.0 copy-done.3
  (1 shorter events, 0.0 us)
Async XLA Ops:
  0.6 19.3 %copy-start.2 = (f32[6144]{0:T(1024)S(1)}, f32[6144]{0:T(1024)}, u32[]{:S(2)}) copy-start(f32[6144]{0:T(1024)} %param.10) | copy-start | bytes 73732
  0.6 19.2 %copy-start = (bf16[6144,1024]{1,0:T(8,128)(2,1)S(1)}, bf16[6144,1024]{1,0:T(8,128)(2,1)}, u32[]{:S(2)}) copy-start(bf16[6144,1024]{1,0:T(8,128)(2,1)} %quant_ref.1) | copy-start | bytes 37748740
  0.7 19.2 %copy-start.1 = (s32[6144,32]{0,1:T(8,128)S(1)}, s32[6144,32]{0,1:T(8,128)}, u32[]{:S(2)}) copy-start(s32[6144,32]{0,1:T(8,128)} %param.8) | copy-start | bytes 2359300
  34.4 0.7 %copy-start.3 = (f32[4,128]{1,0:T(4,128)}, f32[4,128]{1,0:T(4,128)S(1)}, u32[]{:S(2)}) copy-start(f32[4,128]{1,0:T(4,128)S(1)} %reduce_sum.9) | copy-start | bytes 6148

commit v5 on v4

--- a/solution.py
+++ b/solution.py
@@ -24,13 +24,7 @@
     return pltpu.with_memory_space_constraint(x, pltpu.HBM)
 
 
-def pack_kernel(share, q_hbm, cand_hbm, len_hbm, edges_hbm, out_ref, table_ref, q_ref, cand_ref, len_ref, edges_ref, sems):
-    pairs = [(q_hbm, q_ref), (cand_hbm, cand_ref), (len_hbm, len_ref), (edges_hbm, edges_ref)]
-    moves = [pltpu.make_async_copy(*pair, sems.at[n]) for n, pair in enumerate(pairs)]
-    for move in moves:
-        move.start()
-    for move in moves:
-        move.wait()
+def pack_kernel(share, q_ref, cand_ref, len_ref, out_ref):
     own, width = q_ref.shape
     slots = cand_ref.shape[1]
     slot = lax.broadcasted_iota(I32, (1, slots), 1)
@@ -47,16 +41,6 @@
     rows = block.shape[0]
     for p in range(out_ref.shape[0] // rows):
         out_ref[p * rows : (p + 1) * rows, :] = block
-    nbins = edges_ref.shape[0] - 1
-    floor = edges_ref[0] - 1
-    dist = lax.broadcasted_iota(I32, (8, LANES), 1) + floor
-    for j in range(-(-nbins // 4)):
-        word = jnp.zeros((8, LANES), I32)
-        for k in range(4 * j, min(4 * j + 4, nbins)):
-            inside = (dist >= edges_ref[k]) & (dist < edges_ref[k + 1])
-            word = word + jnp.where(inside, jnp.int32(1 << (8 * (k - 4 * j))), 0)
-        table_ref[8 * j : 8 * j + 8, :] = word
-    table_ref[-8:, :] = jnp.full((8, LANES), width // 2 - floor, I32)
 
 
 def unpack(word):
@@ -71,22 +55,29 @@
     return blocks
 
 
-def main_kernel(share, group, cols, nbins, table_ref, x_ref, codes_ref, quant_ref, scale_ref, out_ref, signs_s, qhl_s, bits_s, place_s):
+def main_kernel(share, group, cols, edges_ref, x_ref, codes_ref, quant_ref, scale_ref, out_ref, signs_s, qhl_s, bits_s, place_s):
     count, width = quant_ref.shape
     vregs = width // LANES
     rows = share * vregs + share // 2
     sources = x_ref.shape[0] // rows
     nq = group * share
+    nbins = edges_ref.shape[1] - 1
     src = lax.broadcasted_iota(I32, (2 * TILE, TILE), 0)
     dst = lax.broadcasted_iota(I32, (2 * TILE, TILE), 1)
     perms = [jnp.where(src == (dst & 15) * 32 + 16 * h + (dst >> 4), 1.0, 0.0).astype(BF16) for h in range(2)]
     lane = lax.broadcasted_iota(I32, (LANES, LANES), 1)
     for k in range(nbins):
         place_s[k * LANES : (k + 1) * LANES, :] = jnp.where(lane == LANES // 2 + k, 1.0, 0.0).astype(BF16)
-    tables = [
-        jnp.concatenate([table_ref[8 * j : 8 * j + 8, :]] * (nq // 8), axis=0) for j in range(table_ref.shape[0] // 8 - 1)
-    ]
-    offset = jnp.concatenate([table_ref[-8:, :].astype(F32)] * (nq // 8), axis=0)
+    edge = [jnp.broadcast_to(edges_ref[:, k : k + 1], (8, LANES)) for k in range(nbins + 1)]
+    dist = lax.broadcasted_iota(I32, (8, LANES), 1) + edge[0] - 1
+    tables = []
+    for j in range(-(-nbins // 4)):
+        word = jnp.zeros((8, LANES), I32)
+        for k in range(4 * j, min(4 * j + 4, nbins)):
+            inside = (dist >= edge[k]) & (dist < edge[k + 1])
+            word = word + jnp.where(inside, jnp.int32(1 << (8 * (k - 4 * j))), 0)
+        tables.append(jnp.concatenate([word] * (nq // 8), axis=0))
+    offset = jnp.concatenate([(width // 2 + 1 - edge[0]).astype(F32)] * (nq // 8), axis=0)
 
     def serve(start):
         lane = lax.broadcasted_iota(I32, (group, LANES), 1)
@@ -164,28 +155,18 @@
     assert own % (2 * cores) == 0
     assert words % 16 == 0 and width == 32 * words and count % 512 == 0
     assert count // LANES < 256 and slots <= LANES // 2 and nbins <= LANES // 2
-    payload, table = pl.pallas_call(
+    payload = pl.pallas_call(
         functools.partial(pack_kernel, share),
-        in_specs=[ANY, ANY, ANY, ANY],
-        out_specs=[VMEM, VMEM],
-        out_shape=[
-            pltpu.VMEM((devices * rows, LANES), F32),
-            pltpu.VMEM((8 * -(-nbins // 4) + 8, LANES), I32),
-        ],
-        scratch_shapes=[
-            pltpu.VMEM(queries.shape, F32),
-            pltpu.VMEM(candidates.shape, I32),
-            pltpu.SMEM(shortlist.shape, I32),
-            pltpu.SMEM(edges.shape, I32),
-            pltpu.SemaphoreType.DMA((4,)),
-        ],
+        in_specs=[VMEM, VMEM, SMEM],
+        out_specs=VMEM,
+        out_shape=pltpu.VMEM((devices * rows, LANES), F32),
         compiler_params=pltpu.CompilerParams(vmem_limit_bytes=2 << 20),
         cost_estimate=pl.CostEstimate(flops=10**10, bytes_accessed=0, transcendentals=0),
         name="pack",
-    )(far(queries), far(candidates), far(shortlist), far(edges))
+    )(far(queries), far(candidates), far(shortlist))
     got = lax.all_to_all(payload.reshape(devices, 1, rows * LANES), both, 0, 0).reshape(devices * rows, LANES)
     result = pl.pallas_call(
-        functools.partial(main_kernel, share, group, cols, nbins),
+        functools.partial(main_kernel, share, group, cols),
         in_specs=[VMEM, VMEM, VMEM, VMEM, VMEM],
         out_specs=VMEM,
         out_shape=pltpu.VMEM((nq, LANES), F32),
@@ -198,7 +179,7 @@
         compiler_params=pltpu.CompilerParams(vmem_limit_bytes=24 << 20),
         cost_estimate=pl.CostEstimate(flops=4 * 10**9, bytes_accessed=0, transcendentals=0),
         name="main",
-    )(near(table), near(got), codes.T, quant_rows, row_scale.reshape(1, count))
+    )(near(edges.reshape(1, nbins + 1)), near(got), codes.T, quant_rows, row_scale.reshape(1, count))
     back = lax.all_to_all(result.reshape(devices, 1, share * LANES), both, 0, 0)
     total = jnp.sum(back.reshape(chips, own, LANES), axis=0)
     hist = total[:, LANES // 2 : LANES // 2 + nbins] * (nbins / (count * chips))

time: 35.3 us -> 35.2 us (level)
  no operation moved by 1% of the time
where the time goes in v5:
time: 35.2 us; the launch traced here: 35.1 us
  blocking collectives  27.5 us (78%)
  Pallas kernels  6.16 us (18%)
  between operations  0.69 us (2%)
  other arithmetic  0.68 us (2%)
    all_to_all x1, blocking collectives, shards(): lax.all_to_all(payload.reshape(devices, 1, rows * LANES), both, 0, 0)  18.2 us
    all_to_all x1, blocking collectives, shards(): back = lax.all_to_all(result.reshape(devices, 1, share * LANES), both, 0, 0)  9.31 us
    pallas_call x1, Pallas kernels, shards(): pl.pallas_call(functools.partial(main_kernel, share, group, cols), in_spe...  5.19 us
    pallas_call x1, Pallas kernels, shards(): pl.pallas_call(functools.partial(pack_kernel, share), in_specs=[VMEM, VME...  0.97 us

profile of v5, /device:TPU:0, one launch (start us, length us, event | category | flops | bytes accessed | tf_op | source)
XLA Modules:
  0.0 35.1 jit_solution(16155304287021085241)
XLA Ops:
  0.6 0.0 copy-start.3
  0.6 0.0 copy-start.2
  0.7 0.0 copy-start
  0.7 0.0 copy-start.1
  0.7 1.0 %pack.1 = f32[544,128]{1,0:T(8,128)S(1)} custom-call(f32[4,1024]{1,0:T(4,128)} %q_ref.1, s32[4,40]{1,0:T(4,128)} %cand_ref.1, s32[4]{0:T(128)} %len_ref.1), custom_call_target="tpu_custom_call" | custom-call | flops 10000000000 | tf_op jit(solution)/shard_map/pack/pallas_call | solution.py:158
  1.6 18.2 %all_to_all.10 = f32[32,1,2176]{2,1,0:T(1,128)S(1)} all-to-all(f32[32,1,2176]{2,1,0:T(1,128)S(1)} %bitcast.9), channel_id=1, replica_groups=mesh['corpus'=16,'batch'=2] {'corpus','batch'}, dimensions={0} | all-to-all | bytes 557056 | tf_op jit(solution)/shard_map/all_to_all | solution.py:167
  19.8 0.0 copy-done.3
  19.9 0.0 copy-done.2
  19.9 0.0 copy-done
  19.9 0.0 copy-done.1
  19.9 5.2 %main.1 = f32[64,128]{1,0:T(8,128)S(1)} custom-call(s32[1,17]{1,0:T(1,128)S(1)} %bitcast.13, f32[544,128]{1,0:T(8,128)S(1)} %bitcast.8, s32[32,6144]{1,0:T(8,128)S(1)} %bitcast.11, bf16[6144,1024]{1,0:T(8,128)(2,1)S(1)} %copy-done, f32[1,6144]{1,0:T(1,128)S(1)} %bitcast.12), custom_call_target="tpu_custom_call" | custom-call | flops 4000000000 | tf_op jit(solution)/shard_map/main/pallas_call | solution.py:168
  25.1 9.3 %all_to_all.11 = f32[32,1,256]{2,1,0:T(1,128)S(1)} all-to-all(f32[32,1,256]{2,1,0:T(1,128)S(1)} %bitcast.10), channel_id=1, replica_groups=mesh['corpus'=16,'batch'=2] {'corpus','batch'}, dimensions={0} | all-to-all | bytes 65536 | tf_op jit(solution)/shard_map/all_to_all | solution.py:183
  34.4 0.0 copy-start.4
  34.4 0.7 %slice_multiply_fusion = f32[4,16]{1,0:T(4,128)} fusion(f32[4,128]{1,0:T(4,128)S(1)} %reduce_sum.9), kind=kLoop, calls=%fused_computation | loop fusion | flops 64 | bytes 512 | tf_op jit(solution)/shard_map/mul | solution.py:185
  35.1 0.0 copy-done.4
  (1 shorter events, 0.0 us)
Async XLA Ops:
  0.6 19.2 %copy-start.3 = (s32[17]{0:T(128)S(1)}, s32[17]{0:T(128)}, u32[]{:S(2)}) copy-start(s32[17]{0:T(128)} %param.13) | copy-start | bytes 208
  0.6 19.2 %copy-start.2 = (f32[6144]{0:T(1024)S(1)}, f32[6144]{0:T(1024)}, u32[]{:S(2)}) copy-start(f32[6144]{0:T(1024)} %param.10) | copy-start | bytes 73732
  0.7 19.2 %copy-start = (bf16[6144,1024]{1,0:T(8,128)(2,1)S(1)}, bf16[6144,1024]{1,0:T(8,128)(2,1)}, u32[]{:S(2)}) copy-start(bf16[6144,1024]{1,0:T(8,128)(2,1)} %quant_ref.1) | copy-start | bytes 37748740
  0.7 19.2 %copy-start.1 = (s32[6144,32]{0,1:T(8,128)S(1)}, s32[6144,32]{0,1:T(8,128)}, u32[]{:S(2)}) copy-start(s32[6144,32]{0,1:T(8,128)} %param.8) | copy-start | bytes 2359300
  34.4 0.7 %copy-start.4 = (f32[4,128]{1,0:T(4,128)}, f32[4,128]{1,0:T(4,128)S(1)}, u32[]{:S(2)}) copy-start(f32[4,128]{1,0:T(4,128)S(1)} %reduce_sum.9) | copy-start | bytes 6148

commit v6 on v5

--- a/solution.py
+++ b/solution.py
@@ -161,9 +161,18 @@
         out_specs=VMEM,
         out_shape=pltpu.VMEM((devices * rows, LANES), F32),
         compiler_params=pltpu.CompilerParams(vmem_limit_bytes=2 << 20),
-        cost_estimate=pl.CostEstimate(flops=10**10, bytes_accessed=0, transcendentals=0),
         name="pack",
     )(far(queries), far(candidates), far(shortlist))
+    payload = pl.pallas_call(
+        lambda x_ref, out_ref: None,
+        in_specs=[VMEM],
+        out_specs=VMEM,
+        out_shape=pltpu.VMEM((devices * rows, LANES), F32),
+        input_output_aliases={0: 0},
+        compiler_params=pltpu.CompilerParams(vmem_limit_bytes=1 << 20),
+        cost_estimate=pl.CostEstimate(flops=10**10, bytes_accessed=0, transcendentals=0),
+        name="gate",
+    )(near(payload))
     got = lax.all_to_all(payload.reshape(devices, 1, rows * LANES), both, 0, 0).reshape(devices * rows, LANES)
     result = pl.pallas_call(
         functools.partial(main_kernel, share, group, cols),

time: 35.2 us -> 35.3 us (level)
  no operation moved by 1% of the time
where the time goes in v6:
time: 35.3 us; the launch traced here: 35 us
  blocking collectives  27.5 us (78%)
  Pallas kernels  6.08 us (17%)
  between operations  0.69 us (2%)
  other arithmetic  0.68 us (2%)
    all_to_all x1, blocking collectives, shards(): lax.all_to_all(payload.reshape(devices, 1, rows * LANES), both, 0, 0)  18.2 us
    all_to_all x1, blocking collectives, shards(): back = lax.all_to_all(result.reshape(devices, 1, share * LANES), both, 0, 0)  9.31 us
    pallas_call x1, Pallas kernels, shards(): pl.pallas_call(functools.partial(main_kernel, share, group, cols), in_spe...  5.19 us
    pallas_call x1, Pallas kernels, shards(): pl.pallas_call(functools.partial(pack_kernel, share), in_specs=[VMEM, VME...  0.88 us

profile of v6, /device:TPU:0, one launch (start us, length us, event | category | flops | bytes accessed | tf_op | source)
XLA Modules:
  0.0 35.0 jit_solution(1397032118817288475)
XLA Ops:
  0.6 0.9 %pack.1.x_ref = f32[544,128]{1,0:T(8,128)S(1)} custom-call(f32[4,1024]{1,0:T(4,128)} %q_ref.1, s32[4,40]{1,0:T(4,128)} %cand_ref.1, s32[4]{0:T(128)} %len_ref.1), custom_call_target="tpu_custom_call" | custom-call | tf_op jit(solution)/shard_map/pack/pallas_call | solution.py:158
  1.5 0.0 copy-start
  1.5 0.0 copy-start.1
  1.5 0.0 copy-start.2
  1.6 0.0 copy-start.3
  1.6 18.2 %all_to_all.10 = f32[32,1,2176]{2,1,0:T(1,128)S(1)} all-to-all(f32[32,1,2176]{2,1,0:T(1,128)S(1)} %bitcast.8), channel_id=1, replica_groups=mesh['corpus'=16,'batch'=2] {'corpus','batch'}, dimensions={0} | all-to-all | bytes 557056 | tf_op jit(solution)/shard_map/all_to_all | solution.py:176
  19.8 0.0 copy-done
  19.8 0.0 copy-done.1
  19.8 0.0 copy-done.2
  19.8 0.0 copy-done.3
  19.8 5.2 %main.1 = f32[64,128]{1,0:T(8,128)S(1)} custom-call(s32[1,17]{1,0:T(1,128)S(1)} %bitcast.13, f32[544,128]{1,0:T(8,128)S(1)} %bitcast.9, s32[32,6144]{1,0:T(8,128)S(1)} %bitcast.11, bf16[6144,1024]{1,0:T(8,128)(2,1)S(1)} %copy-done, f32[1,6144]{1,0:T(1,128)S(1)} %bitcast.12), custom_call_target="tpu_custom_call" | custom-call | flops 4000000000 | tf_op jit(solution)/shard_map/main/pallas_call | solution.py:177
  25.0 9.3 %all_to_all.11 = f32[32,1,256]{2,1,0:T(1,128)S(1)} all-to-all(f32[32,1,256]{2,1,0:T(1,128)S(1)} %bitcast.10), channel_id=1, replica_groups=mesh['corpus'=16,'batch'=2] {'corpus','batch'}, dimensions={0} | all-to-all | bytes 65536 | tf_op jit(solution)/shard_map/all_to_all | solution.py:192
  34.3 0.0 copy-start.4
  34.3 0.7 %slice_multiply_fusion = f32[4,16]{1,0:T(4,128)} fusion(f32[4,128]{1,0:T(4,128)S(1)} %reduce_sum.9), kind=kLoop, calls=%fused_computation | loop fusion | flops 64 | bytes 512 | tf_op jit(solution)/shard_map/mul | solution.py:194
  35.0 0.0 copy-done.4
  (2 shorter events, 0.0 us)
Async XLA Ops:
  1.5 18.3 %copy-start = (bf16[6144,1024]{1,0:T(8,128)(2,1)S(1)}, bf16[6144,1024]{1,0:T(8,128)(2,1)}, u32[]{:S(2)}) copy-start(bf16[6144,1024]{1,0:T(8,128)(2,1)} %quant_ref.1) | copy-start | bytes 37748740
  1.5 18.3 %copy-start.1 = (s32[6144,32]{0,1:T(8,128)S(1)}, s32[6144,32]{0,1:T(8,128)}, u32[]{:S(2)}) copy-start(s32[6144,32]{0,1:T(8,128)} %param.8) | copy-start | bytes 2359300
  1.5 18.2 %copy-start.2 = (f32[6144]{0:T(1024)S(1)}, f32[6144]{0:T(1024)}, u32[]{:S(2)}) copy-start(f32[6144]{0:T(1024)} %param.10) | copy-start | bytes 73732
  1.6 18.2 %copy-start.3 = (s32[17]{0:T(128)S(1)}, s32[17]{0:T(128)}, u32[]{:S(2)}) copy-start(s32[17]{0:T(128)} %param.13) | copy-start | bytes 208
  34.3 0.7 %copy-start.4 = (f32[4,128]{1,0:T(4,128)}, f32[4,128]{1,0:T(4,128)S(1)}, u32[]{:S(2)}) copy-start(f32[4,128]{1,0:T(4,128)S(1)} %reduce_sum.9) | copy-start | bytes 6148

commit v7 on v5

--- a/solution.py
+++ b/solution.py
@@ -137,6 +137,15 @@
         serve(0)
     else:
         pl.loop(0, sources // group)(lambda g: serve(g * group))
+
+
+def finish_kernel(unit, back_ref, hist_ref, scores_ref):
+    own, nbins = hist_ref.shape
+    total = jnp.zeros((own, LANES), F32)
+    for c in range(back_ref.shape[0] // own):
+        total = total + back_ref[c * own : (c + 1) * own, :]
+    hist_ref[...] = total[:, LANES // 2 : LANES // 2 + nbins] * unit
+    scores_ref[...] = total[:, : scores_ref.shape[1]]
 
 
 def shards(chips, cores, queries, codes, quant_rows, row_scale, candidates, shortlist, edges):
@@ -181,9 +190,13 @@
         name="main",
     )(near(edges.reshape(1, nbins + 1)), near(got), codes.T, quant_rows, row_scale.reshape(1, count))
     back = lax.all_to_all(result.reshape(devices, 1, share * LANES), both, 0, 0)
-    total = jnp.sum(back.reshape(chips, own, LANES), axis=0)
-    hist = total[:, LANES // 2 : LANES // 2 + nbins] * (nbins / (count * chips))
-    return hist, total[:, :slots]
+    return pl.pallas_call(
+        functools.partial(finish_kernel, nbins / (count * chips)),
+        in_specs=[VMEM],
+        out_specs=[VMEM, VMEM],
+        out_shape=[jax.ShapeDtypeStruct((own, nbins), F32), jax.ShapeDtypeStruct((own, slots), F32)],
+        name="finish",
+    )(near(back.reshape(nq, LANES)))
 
 
 def solution(mesh):

time: 35.2 us -> 35.2 us (level)
  other arithmetic: 0.68 us -> 0 us
  Pallas kernels: 6.16 us -> 6.82 us
    pallas_call x0 -> x1, Pallas kernels: none -> 0.66 us  [shards(): pl.pallas_call(functools.partial(finish_kernel, nbins / (count * chips)),...]
    mul x1 -> x0, other arithmetic: 0.65 us -> none  [shards(): hist = total[:, LANES // 2:LANES // 2 + nbins] * (nbins / (count * chips))]
where the time goes in v7:
time: 35.2 us; the launch traced here: 35 us
  blocking collectives  27.5 us (78%)
  Pallas kernels  6.82 us (19%)
  between operations  0.68 us (2%)
    all_to_all x1, blocking collectives, shards(): lax.all_to_all(payload.reshape(devices, 1, rows * LANES), both, 0, 0)  18.2 us
    all_to_all x1, blocking collectives, shards(): back = lax.all_to_all(result.reshape(devices, 1, share * LANES), both, 0, 0)  9.31 us
    pallas_call x1, Pallas kernels, shards(): pl.pallas_call(functools.partial(main_kernel, share, group, cols), in_spe...  5.19 us
    pallas_call x1, Pallas kernels, shards(): pl.pallas_call(functools.partial(pack_kernel, share), in_specs=[VMEM, VME...  0.97 us

profile of v7, /device:TPU:0, one launch (start us, length us, event | category | flops | bytes accessed | tf_op | source)
XLA Modules:
  0.0 35.0 jit_solution(16013919259600247637)
XLA Ops:
  0.6 0.0 copy-start.3
  0.6 0.0 copy-start.2
  0.7 0.0 copy-start
  0.7 0.0 copy-start.1
  0.7 1.0 %pack.1 = f32[544,128]{1,0:T(8,128)S(1)} custom-call(f32[4,1024]{1,0:T(4,128)} %q_ref.1, s32[4,40]{1,0:T(4,128)} %cand_ref.1, s32[4]{0:T(128)} %len_ref.1), custom_call_target="tpu_custom_call" | custom-call | flops 10000000000 | tf_op jit(solution)/shard_map/pack/pallas_call | solution.py:167
  1.6 18.2 %all_to_all.10 = f32[32,1,2176]{2,1,0:T(1,128)S(1)} all-to-all(f32[32,1,2176]{2,1,0:T(1,128)S(1)} %bitcast.8), channel_id=1, replica_groups=mesh['corpus'=16,'batch'=2] {'corpus','batch'}, dimensions={0} | all-to-all | bytes 557056 | tf_op jit(solution)/shard_map/all_to_all | solution.py:176
  19.8 0.0 copy-done.3
  19.9 0.0 copy-done.2
  19.9 0.0 copy-done
  19.9 0.0 copy-done.1
  19.9 5.2 %main.1 = f32[64,128]{1,0:T(8,128)S(1)} custom-call(s32[1,17]{1,0:T(1,128)S(1)} %bitcast.13, f32[544,128]{1,0:T(8,128)S(1)} %bitcast.7, s32[32,6144]{1,0:T(8,128)S(1)} %bitcast.11, bf16[6144,1024]{1,0:T(8,128)(2,1)S(1)} %copy-done, f32[1,6144]{1,0:T(1,128)S(1)} %bitcast.12), custom_call_target="tpu_custom_call" | custom-call | flops 4000000000 | tf_op jit(solution)/shard_map/main/pallas_call | solution.py:177
  25.1 9.3 %all_to_all.11 = f32[32,1,256]{2,1,0:T(1,128)S(1)} all-to-all(f32[32,1,256]{2,1,0:T(1,128)S(1)} %bitcast.10), channel_id=1, replica_groups=mesh['corpus'=16,'batch'=2] {'corpus','batch'}, dimensions={0} | all-to-all | bytes 65536 | tf_op jit(solution)/shard_map/all_to_all | solution.py:192
  34.4 0.7 %finish.1 = (f32[4,16]{1,0:T(4,128)}, f32[4,40]{1,0:T(4,128)}) custom-call(f32[64,128]{1,0:T(8,128)S(1)} %bitcast.9), custom_call_target="tpu_custom_call" | custom-call | tf_op jit(solution)/shard_map/finish/pallas_call | solution.py:193
Async XLA Ops:
  0.6 19.2 %copy-start.3 = (s32[17]{0:T(128)S(1)}, s32[17]{0:T(128)}, u32[]{:S(2)}) copy-start(s32[17]{0:T(128)} %param.13) | copy-start | bytes 208
  0.6 19.2 %copy-start.2 = (f32[6144]{0:T(1024)S(1)}, f32[6144]{0:T(1024)}, u32[]{:S(2)}) copy-start(f32[6144]{0:T(1024)} %param.10) | copy-start | bytes 73732
  0.7 19.2 %copy-start = (bf16[6144,1024]{1,0:T(8,128)(2,1)S(1)}, bf16[6144,1024]{1,0:T(8,128)(2,1)}, u32[]{:S(2)}) copy-start(bf16[6144,1024]{1,0:T(8,128)(2,1)} %quant_ref.1) | copy-start | bytes 37748740
  0.7 19.2 %copy-start.1 = (s32[6144,32]{0,1:T(8,128)S(1)}, s32[6144,32]{0,1:T(8,128)}, u32[]{:S(2)}) copy-start(s32[6144,32]{0,1:T(8,128)} %param.8) | copy-start | bytes 2359300
